TPU v7x, 128 devices: a whole 4x4x4 slice. The times are simulated.
128 devices in a mesh: dp: 1, row: 16 (over z, y), col: 8 (over x, core).
Axes of the slice: x: 4, y: 4, z: 4, core: 2. Of those that a mesh axis runs over, the one named last changes fastest.
Arguments:
- x_in: bfloat16 [16, 512, 4096], P('dp', None, ('row', 'col'))
- ln_gain: bfloat16 [2, 4096], P(None, ('row', 'col'))
- w_in: bfloat16 [2, 4096, 36864], P(None, 'row', 'col')
- w_kv: bfloat16 [2, 4096, 256], P(None, 'row', 'col')
- w_out: bfloat16 [2, 20480, 4096], P(None, 'col', 'row')
Outputs:
- output 1: bfloat16 [16, 512, 4096], P('dp', None, ('row', 'col'))
- output 2: bfloat16 [2, 2, 16, 512, 128], P(None, None, 'dp', ('row', 'col'))
All inputs are finite; a program needn't handle non-finite values.
Results may differ from a plain program's by a relative error of at most 0.0180243.
Values are sent between devices in bfloat16 or wider.
A program may use at most 1 GiB of HBM per device.

v0:
```python
import jax
import jax.numpy as jnp
from jax import lax
from jax.sharding import PartitionSpec as P

LN_EPS = 1e-6


def rope_tables(positions, head_dim):
    half_dim = head_dim // 2
    inv_freq = 1.0 / (10000.0 ** (jnp.arange(half_dim, dtype=jnp.float32) * 2.0 / head_dim))
    angles = positions.astype(jnp.float32)[:, None] * inv_freq[None, :]
    return jnp.cos(angles), jnp.sin(angles)


def apply_rope(values, cos_tab, sin_tab):
    half_dim = values.shape[-1] // 2
    lower_half = values[..., :half_dim]
    upper_half = values[..., half_dim:]
    return jnp.concatenate([lower_half * cos_tab - upper_half * sin_tab, upper_half * cos_tab + lower_half * sin_tab], axis=-1)


def solution(mesh):
    row_size = mesh.shape["row"]
    col_size = mesh.shape["col"]
    act_spec = P("dp", None, ("row", "col"))
    weight_spec = P(None, "row", "col")

    def device_fn(x_loc, gain_loc, w_in_loc, w_kv_loc, w_out_loc):
        n_layers = w_in_loc.shape[0]
        n_batch, seq_len, d_local = x_loc.shape
        d_model = d_local * row_size * col_size
        e_block = w_in_loc.shape[2]
        r_block = w_out_loc.shape[1]
        f_block = e_block - r_block
        q_block = r_block - f_block
        head_dim = w_kv_loc.shape[2] * col_size // 2
        heads_local = q_block // head_dim
        seq_local = seq_len // (row_size * col_size)
        shard_index = lax.axis_index("row") * col_size + lax.axis_index("col")
        positions = jnp.arange(seq_len)
        cos_tab, sin_tab = rope_tables(positions, head_dim)
        causal = positions[None, :] <= positions[:, None]
        hidden = x_loc
        kv_outs = []
        for layer_idx in range(n_layers):
            hidden_f32 = hidden.astype(jnp.float32)
            tok_sum = lax.psum(jnp.sum(hidden_f32, axis=-1, keepdims=True), ("row", "col"))
            centered = hidden_f32 - tok_sum / d_model
            sq_sum = lax.psum(jnp.sum(centered * centered, axis=-1, keepdims=True), ("row", "col"))
            normed = (centered * lax.rsqrt(sq_sum / d_model + LN_EPS) * gain_loc[layer_idx].astype(jnp.float32)).astype(jnp.bfloat16)
            normed_row = lax.all_gather(normed, "col", axis=2, tiled=True)
            part_main = jnp.einsum("bsd,de->bse", normed_row, w_in_loc[layer_idx], preferred_element_type=jnp.float32).astype(jnp.bfloat16)
            part_kv = jnp.einsum("bsd,de->bse", normed_row, w_kv_loc[layer_idx], preferred_element_type=jnp.float32).astype(jnp.bfloat16)
            main_proj, kv_piece = lax.psum((part_main, part_kv), "row")
            kv_proj = lax.all_gather(kv_piece, "col", axis=2, tiled=True)
            query = main_proj[..., :q_block].reshape(n_batch, seq_len, heads_local, head_dim)
            gate_val = main_proj[..., q_block:q_block + f_block]
            up_val = main_proj[..., q_block + f_block:]
            q_rot = (apply_rope(query.astype(jnp.float32), cos_tab[:, None, :], sin_tab[:, None, :]) * head_dim ** -0.5).astype(jnp.bfloat16)
            k_rot = apply_rope(kv_proj[..., :head_dim].astype(jnp.float32), cos_tab, sin_tab).astype(jnp.bfloat16)
            v_val = kv_proj[..., head_dim:]
            scores = jnp.einsum("crie,cle->cirl", q_rot, k_rot, preferred_element_type=jnp.float32)
            scores = jnp.where(causal, scores, -1e30)
            attn_prob = jax.nn.softmax(scores, axis=-1).astype(jnp.bfloat16)
            attn_out = jnp.einsum("cirl,cle->crie", attn_prob, v_val, preferred_element_type=jnp.float32).astype(jnp.bfloat16).reshape(n_batch, seq_len, q_block)
            mlp_out = (jax.nn.silu(gate_val.astype(jnp.float32)) * up_val.astype(jnp.float32)).astype(jnp.bfloat16)
            joined = jnp.concatenate([attn_out, mlp_out], axis=2)
            part_out = jnp.einsum("bsr,rd->bsd", joined, w_out_loc[layer_idx], preferred_element_type=jnp.float32).astype(jnp.bfloat16)
            update = lax.psum_scatter(part_out, "col", scatter_dimension=2, tiled=True)
            hidden = hidden + update
            kv_outs.append(lax.dynamic_slice_in_dim(jnp.stack([k_rot, v_val]), shard_index * seq_local, seq_local, axis=2))
        return hidden, jnp.stack(kv_outs)

    return jax.shard_map(device_fn, mesh=mesh, in_specs=(act_spec, P(None, ("row", "col")), weight_spec, weight_spec, P(None, "col", "row")), out_specs=(act_spec, P(None, None, "dp", ("row", "col"), None)), check_vma=False)
```

profile of v0, /device:TPU:1, one launch (start us, length us, event | category | flops | bytes accessed | tf_op | source)
XLA Modules:
  0.0 2652.4 jit_solution(4659886507072849151)
XLA Ops:
  7.2 1.2 bitcast_convert_fusion
  8.5 1.2 convert_reduce_fusion.1
  9.6 68.9 %psum.56 = f32[16,512,1]{1,0,2:T(8,128)S(1)} all-reduce(f32[16,512,1]{1,0,2:T(8,128)S(1)} %bitcast.119), channel_id=1, replica_groups=mesh['dp'=1,'row'=16,'col'=8] {'row','col'}, use_global_device_ids=true, to_apply=%region_1.0 | all-reduce | flops 8192 | bytes 65536 | tf_op jit(solution)/shard_map/psum | solution.py:48
  78.5 1.2 fusion.67
  79.7 62.6 %psum.57 = f32[16,512,1]{1,0,2:T(8,128)S(1)} all-reduce(f32[16,512,1]{1,0,2:T(8,128)S(1)} %bitcast.120), channel_id=1, replica_groups=mesh['dp'=1,'row'=16,'col'=8] {'row','col'}, use_global_device_ids=true, to_apply=%region_3.0 | all-reduce | flops 8192 | bytes 65536 | tf_op jit(solution)/shard_map/psum | solution.py:50
  142.3 2.0 fusion.69
  144.4 29.7 %all-gather.5.cloned.1.call-done = bf16[16,512,256]{1,2,0:T(8,128)(2,1)} async-done(((bf16[16,512,32]{1,2,0:T(8,128)(2,1)}), bf16[16,512,256]{1,2,0:T(8,128)(2,1)}) %all-gather.5.cloned.1.call-update) | async-done | bytes 4194320 | tf_op jit(solution)/shard_map/all_gather | solution.py:52
  174.1 3.8 convolution_convert_fusion.3
  177.9 30.9 %convolution_convert_fusion.1 = bf16[16,512,4608]{2,1,0:T(8,128)(2,1)} fusion(bf16[16,512,256]{1,2,0:T(8,128)(2,1)} %all-gather.5.cloned.1.call-done, bf16[2,256,4608]{2,1,0:T(8,128)(2,1)} %param.7), kind=kOutput, calls=%fused_computation.25 | convolution fusion | flops 19365101568 | bytes 82051072 | tf_op jit(solution)/shard_map/bsd,de->bse/dot_general | solution.py:53
  209.8 814.2 %all-reduce.7.cloned.1.call-done = (bf16[16,512,4608]{2,1,0:T(8,128)(2,1)}, bf16[16,512,32]{1,2,0:T(8,128)(2,1)}) async-done(((bf16[16,512,4608]{2,1,0:T(8,128)(2,1)}, bf16[16,512,32]{1,2,0:T(8,128)(2,1)}), (bf16[16,512,4608]{2,1,0:T(8,128)(2,1)}, bf16[16,512,32]{1,2,0:T(8,128)(2,1)})) %all-reduce.7.cloned.1.call-update) | async-done | bytes 76021776 | tf_op jit(solution)/shard_map/psum | solution.py:55
  1024.1 11.5 slice_convert_fusion.1
  1035.6 19.7 reshape.217
  1055.3 22.0 fusion.89
  1077.3 17.8 multiply_subtract_fusion.1
  1095.1 33.8 %fusion.11 = bf16[16,512,2048]{2,1,0:T(8,128)(2,1)} fusion(bf16[16,512,4608]{2,1,0:T(8,128)(2,1)} %get-tuple-element.6), kind=kLoop, calls=%fused_computation.21 | loop fusion | flops 134217728 | bytes 100663296 | tf_op jit(solution)/shard_map/convert_element_type | solution.py:67
  1129.0 4.3 slice_bitcast_fusion.1
  1133.3 0.8 subtract_convert_fusion.1
  1134.1 34.4 %fusion.32 = f32[16,512,512,4]{2,1,3,0:T(8,128)} fusion(f32[16,512,4,64]{3,1,2,0:T(8,128)} %get-tuple-element.13, f32[16,512,4,64]{3,1,2,0:T(8,128)} %get-tuple-element.12, bf16[16,512,64]{1,2,0:T(8,128)(2,1)S(1)} %get-tuple-element.21, bf16[16,512,64]{1,2,0:T(8,128)(2,1)S(1)} %get-tuple-element.20), kind=kOutput, calls=%fused_computation.49 | convolution fusion | flops 4311744512 | bytes 85983232 | tf_op jit(solution)/shard_map/crie,cle->cirl/dot_general | solution.py:63
  1168.5 66.2 %fusion.90 = (f32[16,4,512]{2,1,0:T(4,128)S(1)}, f32[16,4,512,512]{2,3,1,0:T(8,128)}) fusion(f32[16,512,512,4]{2,1,3,0:T(8,128)} %fusion.32, pred[512,512]{0,1:T(8,128)(4,1)S(1)} %iota_compare_fusion), kind=kOutput, calls=%fused_computation.138 | output fusion | flops 67109376 | bytes 134610944 | tf_op jit(solution)/shard_map/sub | solution.py:65
  1234.8 26.2 fusion.37
  1261.0 12.3 copy.46
  1273.2 19.1 fusion.41
  1292.4 35.0 %reduce-scatter.3.cloned.1.call-done = bf16[16,512,32]{1,2,0:T(8,128)(2,1)} async-done(((bf16[16,512,256]{1,2,0:T(8,128)(2,1)}), bf16[16,512,32]{1,2,0:T(8,128)(2,1)}) %reduce-scatter.3.cloned.1.call-update) | async-done | bytes 524304 | tf_op jit(solution)/shard_map/reduce_scatter | solution.py:70
  1327.5 1.3 convert_reduce_fusion
  1328.8 68.1 %psum.60 = f32[16,512,1]{1,0,2:T(8,128)S(1)} all-reduce(f32[16,512,1]{1,0,2:T(8,128)S(1)} %bitcast.118), channel_id=1, replica_groups=mesh['dp'=1,'row'=16,'col'=8] {'row','col'}, use_global_device_ids=true, to_apply=%region_10.11 | all-reduce | flops 8192 | bytes 65536 | tf_op jit(solution)/shard_map/psum | solution.py:48
  1397.0 62.5 %psum.61 = f32[16,512,1]{1,0,2:T(8,128)S(1)} all-reduce(f32[16,512,1]{1,0,2:T(8,128)S(1)} %bitcast.121), channel_id=1, replica_groups=mesh['dp'=1,'row'=16,'col'=8] {'row','col'}, use_global_device_ids=true, to_apply=%region_12.13 | all-reduce | flops 8192 | bytes 65536 | tf_op jit(solution)/shard_map/psum | solution.py:50
  1459.6 1.0 fusion.66
  1460.7 29.3 %all-gather.9.cloned.1.call-done = bf16[16,512,256]{1,2,0:T(8,128)(2,1)} async-done(((bf16[16,512,32]{1,2,0:T(8,128)(2,1)}), bf16[16,512,256]{1,2,0:T(8,128)(2,1)}) %all-gather.9.cloned.1.call-update) | async-done | bytes 4194320 | tf_op jit(solution)/shard_map/all_gather | solution.py:52
  1490.0 3.8 convolution_convert_fusion.2
  1493.8 30.9 %convolution_convert_fusion = bf16[16,512,4608]{2,1,0:T(8,128)(2,1)} fusion(bf16[16,512,256]{1,2,0:T(8,128)(2,1)} %all-gather.9.cloned.1.call-done, bf16[2,256,4608]{2,1,0:T(8,128)(2,1)} %param.7), kind=kOutput, calls=%fused_computation.24 | convolution fusion | flops 19365101568 | bytes 82051072 | tf_op jit(solution)/shard_map/bsd,de->bse/dot_general | solution.py:53
  1524.8 815.1 %all-reduce.5.cloned.1.call-done = (bf16[16,512,4608]{2,1,0:T(8,128)(2,1)}, bf16[16,512,32]{1,2,0:T(8,128)(2,1)}) async-done(((bf16[16,512,4608]{2,1,0:T(8,128)(2,1)}, bf16[16,512,32]{1,2,0:T(8,128)(2,1)}), (bf16[16,512,4608]{2,1,0:T(8,128)(2,1)}, bf16[16,512,32]{1,2,0:T(8,128)(2,1)})) %all-reduce.5.cloned.1.call-update) | async-done | bytes 76021776 | tf_op jit(solution)/shard_map/psum | solution.py:55
  2340.2 11.5 slice_convert_fusion
  2351.7 19.2 reshape.219
  2370.9 22.0 fusion.88
  2392.9 17.8 multiply_subtract_fusion
  2410.8 33.9 %fusion.10 = bf16[16,512,2048]{2,1,0:T(8,128)(2,1)} fusion(bf16[16,512,4608]{2,1,0:T(8,128)(2,1)} %get-tuple-element.4), kind=kLoop, calls=%fused_computation.20 | loop fusion | flops 134217728 | bytes 100663296 | tf_op jit(solution)/shard_map/convert_element_type | solution.py:67
  2444.7 4.3 slice_bitcast_fusion
  2449.0 0.8 subtract_convert_fusion
  2449.8 34.1 %fusion.30 = f32[16,512,512,4]{2,1,3,0:T(8,128)} fusion(f32[16,512,4,64]{3,1,2,0:T(8,128)} %get-tuple-element.11, f32[16,512,4,64]{3,1,2,0:T(8,128)} %get-tuple-element.10, bf16[16,512,64]{1,2,0:T(8,128)(2,1)S(1)} %get-tuple-element.19, bf16[16,512,64]{1,2,0:T(8,128)(2,1)S(1)} %get-tuple-element.18), kind=kOutput, calls=%fused_computation.48 | convolution fusion | flops 4311744512 | bytes 85983232 | tf_op jit(solution)/shard_map/crie,cle->cirl/dot_general | solution.py:63
  2483.9 66.2 %fusion.91 = (f32[16,4,512]{2,1,0:T(4,128)S(1)}, f32[16,4,512,512]{2,3,1,0:T(8,128)}) fusion(f32[16,512,512,4]{2,1,3,0:T(8,128)} %fusion.30, pred[512,512]{0,1:T(8,128)(4,1)S(1)} %copy-done.1), kind=kOutput, calls=%fused_computation.139 | output fusion | flops 67109376 | bytes 134610944 | tf_op jit(solution)/shard_map/sub | solution.py:65
  2550.1 26.3 fusion.36
  2576.4 12.3 copy.49
  2588.7 19.2 fusion.38
  2607.9 3.4 fusion.71
  2611.3 1.6 copy.36
  2612.9 1.6 copy.35
  2615.2 27.8 %reduce-scatter.5.cloned.1.call-done = bf16[16,512,32]{1,2,0:T(8,128)(2,1)} async-done(((bf16[16,512,256]{1,2,0:T(8,128)(2,1)}), bf16[16,512,32]{1,2,0:T(8,128)(2,1)}) %reduce-scatter.5.cloned.1.call-update) | async-done | bytes 524304 | tf_op jit(solution)/shard_map/reduce_scatter | solution.py:70
  2643.0 2.2 add.67
  (69 shorter events, 2.6 us)
Async XLA Ops:
  7.2 166.9 %all-gather.5.cloned.1.call-start = ((), (), s32[]{:S(2)}) async-start(), calls=%async_computation.2 | async-start | bytes 4718592 | tf_op jit(solution)/shard_map/all_gather | solution.py:52
  144.4 879.7 %all-reduce.7.cloned.1.call-start = ((), (), s32[]{:S(2)}) async-start(), calls=%async_computation.9 | async-start | bytes 152043520 | tf_op jit(solution)/shard_map/psum | solution.py:55
  208.8 920.2 %all-gather.7.cloned.1.call-start = ((), (), s32[]{:S(2)}) async-start(), calls=%async_computation.3 | async-start | bytes 4718592 | tf_op jit(solution)/shard_map/all_gather | solution.py:56
  209.4 923.9 %copy-start.13 = (f32[512,64]{0,1:T(8,128)}, f32[512,64]{0,1:T(8,128)S(1)}, u32[]{:S(2)}) copy-start(f32[512,64]{0,1:T(8,128)S(1)} %get-tuple-element.26) | copy-start | bytes 393220
  209.4 923.9 %copy-start.15 = (f32[512,64]{0,1:T(8,128)}, f32[512,64]{0,1:T(8,128)S(1)}, u32[]{:S(2)}) copy-start(f32[512,64]{0,1:T(8,128)S(1)} %get-tuple-element.27) | copy-start | bytes 393220
  209.6 867.7 %copy-start.9 = (f32[512,64]{1,0:T(8,128)}, f32[512,64]{1,0:T(8,128)S(1)}, u32[]{:S(2)}) copy-start(f32[512,64]{1,0:T(8,128)S(1)} %copy.22) | copy-start | bytes 393220
  209.7 867.6 %copy-start.11 = (f32[512,64]{1,0:T(8,128)}, f32[512,64]{1,0:T(8,128)S(1)}, u32[]{:S(2)}) copy-start(f32[512,64]{1,0:T(8,128)S(1)} %copy.24) | copy-start | bytes 393220
  209.8 958.7 %copy-start = (pred[512,512]{0,1:T(8,128)(4,1)}, pred[512,512]{0,1:T(8,128)(4,1)S(1)}, u32[]{:S(2)}) copy-start(pred[512,512]{0,1:T(8,128)(4,1)S(1)} %iota_compare_fusion) | copy-start | bytes 786436
  1024.0 303.4 %reduce-scatter.3.cloned.1.call-start = ((), (), s32[]{:S(2)}) async-start(), calls=%async_computation.4 | async-start | bytes 4718592 | tf_op jit(solution)/shard_map/reduce_scatter | solution.py:70
  1134.1 34.4 %copy-start.2 = (bf16[16,512,64]{1,2,0:T(8,128)(2,1)}, bf16[16,512,64]{1,2,0:T(8,128)(2,1)S(1)}, u32[]{:S(2)}) copy-start(bf16[16,512,64]{1,2,0:T(8,128)(2,1)S(1)} %get-tuple-element.20) | copy-start | bytes 3145732
  1134.1 34.4 %copy-start.4 = (bf16[16,512,64]{1,2,0:T(8,128)(2,1)}, bf16[16,512,64]{1,2,0:T(8,128)(2,1)S(1)}, u32[]{:S(2)}) copy-start(bf16[16,512,64]{1,2,0:T(8,128)(2,1)S(1)} %get-tuple-element.21) | copy-start | bytes 3145732
  1273.2 54.2 %copy-start.8 = (bf16[16,512,32]{1,2,0:T(8,128)(2,1)S(1)}, bf16[16,512,32]{1,2,0:T(8,128)(2,1)}, u32[]{:S(2)}) copy-start(bf16[16,512,32]{1,2,0:T(8,128)(2,1)} %param.5) | copy-start | bytes 1572868
  1273.2 186.3 %copy-start.18 = (f32[32]{0:T(128)S(1)}, f32[32]{0:T(128)}, u32[]{:S(2)}) copy-start(f32[32]{0:T(128)} %get-tuple-element.28) | copy-start | bytes 388
  1273.2 216.7 %copy-start.17 = (bf16[2,256,32]{1,2,0:T(8,128)(2,1)S(1)}, bf16[2,256,32]{1,2,0:T(8,128)(2,1)}, u32[]{:S(2)}) copy-start(bf16[2,256,32]{1,2,0:T(8,128)(2,1)} %param.8) | copy-start | bytes 98308
  1292.4 197.6 %all-gather.9.cloned.1.call-start = ((), (), s32[]{:S(2)}) async-start(), calls=%async_computation.5 | async-start | bytes 4718592 | tf_op jit(solution)/shard_map/all_gather | solution.py:52
  1328.8 195.9 %copy-start.7 = (bf16[16,512,32]{1,2,0:T(8,128)(2,1)}, bf16[16,512,32]{1,2,0:T(8,128)(2,1)S(1)}, u32[]{:S(2)}) copy-start(bf16[16,512,32]{1,2,0:T(8,128)(2,1)S(1)} %get-tuple-element.9) | copy-start | bytes 1572868
  1460.6 879.2 %all-reduce.5.cloned.1.call-start = ((), (), s32[]{:S(2)}) async-start(), calls=%async_computation.8 | async-start | bytes 152043520 | tf_op jit(solution)/shard_map/psum | solution.py:55
  1524.7 920.0 %all-gather.11.cloned.1.call-start = ((), (), s32[]{:S(2)}) async-start(), calls=%async_computation.6 | async-start | bytes 4718592 | tf_op jit(solution)/shard_map/all_gather | solution.py:56
  2339.9 303.1 %reduce-scatter.5.cloned.1.call-start = ((), (), s32[]{:S(2)}) async-start(), calls=%async_computation.7 | async-start | bytes 4718592 | tf_op jit(solution)/shard_map/reduce_scatter | solution.py:70
  2370.9 22.0 copy-start.10
  2370.9 22.0 copy-start.12
  2410.8 38.2 %copy-start.14 = (f32[512,64]{0,1:T(8,128)S(1)}, f32[512,64]{0,1:T(8,128)}, u32[]{:S(2)}) copy-start(f32[512,64]{0,1:T(8,128)} %copy-done.13) | copy-start | bytes 393220
  2410.8 38.2 %copy-start.16 = (f32[512,64]{0,1:T(8,128)S(1)}, f32[512,64]{0,1:T(8,128)}, u32[]{:S(2)}) copy-start(f32[512,64]{0,1:T(8,128)} %copy-done.15) | copy-start | bytes 393220
  2449.8 34.1 %copy-start.6 = (bf16[16,512,64]{1,2,0:T(8,128)(2,1)}, bf16[16,512,64]{1,2,0:T(8,128)(2,1)S(1)}, u32[]{:S(2)}) copy-start(bf16[16,512,64]{1,2,0:T(8,128)(2,1)S(1)} %get-tuple-element.19) | copy-start | bytes 3145732
  2449.8 34.1 %copy-start.1 = (pred[512,512]{0,1:T(8,128)(4,1)S(1)}, pred[512,512]{0,1:T(8,128)(4,1)}, u32[]{:S(2)}) copy-start(pred[512,512]{0,1:T(8,128)(4,1)} %copy-done) | copy-start | bytes 786436
  2588.7 19.2 copy-start.3
  2588.7 19.3 copy-start.5
Sparse Core Ops, SparseCore 0:
  144.5 29.5 all-gather.4
  208.9 815.0 all-reduce.6
  1025.7 32.1 all-gather.6
  1292.5 34.9 reduce-scatter.2
  1460.8 29.1 all-gather.8
  1524.8 815.0 all-reduce.4
  2341.6 32.1 all-gather.10
  2608.0 34.9 reduce-scatter.4
where the time goes:
time: 2660 us; the launch traced here: 2650 us
  waiting for transfers between devices  1750 us (66%)
  other arithmetic  283 us (11%)
  blocking collectives  262 us (10%)
  matrix products  229 us (9%)
  local copies, waits for them, and re-layouts  112 us (4%)
    psum x2, waiting for transfers between devices, device_fn(): main_proj, kv_piece = lax.psum((part_main, part_kv), 'row')  1630 us
    psum x2, blocking collectives, device_fn(): lax.psum(jnp.sum(hidden_f32, axis=-1, keepdims=True), ('row', 'col'))  137 us
    sub x2, other arithmetic, device_fn(): attn_prob = jax.nn.softmax(scores, axis=-1).astype(jnp.bfloat16)  132 us
    psum x2, blocking collectives, device_fn(): lax.psum(jnp.sum(centered * centered, axis=-1, keepdims=True), ('row', 'c...  125 us
    dot_general x2, matrix products, device_fn(): jnp.einsum('crie,cle->cirl', q_rot, k_rot, preferred_element_type=jnp.flo...  68.5 us
    convert_element_type x2, other arithmetic, device_fn(): (jax.nn.silu(gate_val.astype(jnp.float32)) * up_val.astype(jnp.float32))....  67.7 us
    reduce_scatter x2, waiting for transfers between devices, device_fn(): update = lax.psum_scatter(part_out, 'col', scatter_dimension=2, tiled=True)  62.8 us
    dot_general x2, matrix products, device_fn(): jnp.einsum('bsd,de->bse', normed_row, w_in_loc[layer_idx], preferred_elem...  61.8 us
  transfers between devices with their start and end apart: 8, of which 6 were waited for; matrix products, arithmetic and copies ran while one was open for 8% of the time, Pallas kernels for 0%

commit v1 on v0

v1 whole, which is shorter than its diff:
```python
import jax
import jax.numpy as jnp
from jax import lax
from jax.sharding import Mesh
from jax.sharding import PartitionSpec as P

LN_EPS = 1e-6
NZ = 4


def rope_tables(positions, head_dim):
    half_dim = head_dim // 2
    inv_freq = 1.0 / (10000.0 ** (jnp.arange(half_dim, dtype=jnp.float32) * 2.0 / head_dim))
    angles = positions.astype(jnp.float32)[:, None] * inv_freq[None, :]
    return jnp.cos(angles), jnp.sin(angles)


def apply_rope(values, cos_tab, sin_tab):
    half_dim = values.shape[-1] // 2
    lower_half = values[..., :half_dim]
    upper_half = values[..., half_dim:]
    return jnp.concatenate([lower_half * cos_tab - upper_half * sin_tab, upper_half * cos_tab + lower_half * sin_tab], axis=-1)


def solution(mesh):
    row_size = mesh.shape["row"]
    n_col = mesh.shape["col"]
    n_z = NZ
    n_y = row_size // n_z
    n_tp = n_y * n_col
    n_dev = row_size * n_col
    mesh4 = Mesh(mesh.devices.reshape(n_z, n_y, n_col), ("z", "y", "col"))
    every = ("z", "y", "col")
    tp = ("y", "col")
    act_spec = P(None, None, every)
    w_spec = P(None, ("z", "y"), "col")

    def device_fn(x_loc, gain_loc, w_in_loc, w_kv_loc, w_out_loc):
        n_layers = w_in_loc.shape[0]
        n_batch, seq_len, d_local = x_loc.shape
        d_model = d_local * n_dev
        e_block = w_in_loc.shape[2]
        r_block = w_out_loc.shape[1]
        f_block = e_block - r_block
        q_block = r_block - f_block
        q_loc, f_loc = q_block // n_y, f_block // n_y
        head_dim = w_kv_loc.shape[2] * n_col // 2
        heads_local = q_loc // head_dim
        batch_loc = n_batch // n_z
        n_tok = n_batch * seq_len
        tok_z = n_tok // n_z
        tok_loc = n_tok // n_dev
        seq_local = seq_len // n_dev
        d_row = w_in_loc.shape[1]
        positions = jnp.arange(seq_len)
        cos_tab, sin_tab = rope_tables(positions, head_dim)
        causal = positions[None, :] <= positions[:, None]

        gain = lax.all_gather(gain_loc, every, axis=1, tiled=True)

        weights = []
        for l in range(n_layers):
            wi = w_in_loc[l]
            q_part = wi[:, :q_block].reshape(d_row, n_y, q_loc)
            g_part = wi[:, q_block:q_block + f_block].reshape(d_row, n_y, f_loc)
            u_part = wi[:, q_block + f_block:].reshape(d_row, n_y, f_loc)
            wi = jnp.concatenate([q_part, g_part, u_part], axis=2).transpose(1, 0, 2)
            wi = lax.all_to_all(wi, "y", 0, 0, tiled=True).reshape(n_y * d_row, q_loc + 2 * f_loc)
            wkv = lax.all_gather(w_kv_loc[l], "col", axis=1, tiled=True)
            wkv = lax.all_gather(wkv, "y", axis=0, tiled=True)
            wi = lax.all_gather(jnp.concatenate([wi, wkv], axis=1), "z", axis=0, tiled=True)
            wo = w_out_loc[l]
            wo = jnp.concatenate([wo[:q_block].reshape(n_y, q_loc, -1), wo[q_block:].reshape(n_y, f_loc, -1)], axis=1)
            wo = lax.all_to_all(wo, "y", 0, 0, tiled=True)
            wo = wo.transpose(1, 0, 2).reshape(q_loc + f_loc, -1)
            wo = lax.all_gather(wo, "z", axis=1, tiled=True)
            weights.append((wi, wo))

        xs = lax.all_to_all(x_loc.reshape(n_dev, tok_loc, d_local), every, 0, 0, tiled=True)
        hidden = xs.reshape(n_dev, tok_loc, d_local).transpose(1, 0, 2).reshape(tok_loc, d_model)
        kv_outs = []
        for l in range(n_layers):
            w_i, w_o = weights[l]
            hf = hidden.astype(jnp.float32)
            mean = jnp.mean(hf, axis=-1, keepdims=True)
            centered = hf - mean
            var = jnp.mean(centered * centered, axis=-1, keepdims=True)
            normed = (centered * lax.rsqrt(var + LN_EPS) * gain[l].astype(jnp.float32)).astype(jnp.bfloat16)
            h = lax.all_gather(normed, tp, axis=0, tiled=True)
            proj = jnp.dot(h, w_i, preferred_element_type=jnp.float32).astype(jnp.bfloat16)
            query = proj[:, :q_loc].reshape(batch_loc, seq_len, heads_local, head_dim)
            gate_val = proj[:, q_loc:q_loc + f_loc]
            up_val = proj[:, q_loc + f_loc:q_loc + 2 * f_loc]
            kv_proj = proj[:, q_loc + 2 * f_loc:].reshape(batch_loc, seq_len, 2 * head_dim)
            q_rot = (apply_rope(query.astype(jnp.float32), cos_tab[:, None, :], sin_tab[:, None, :]) * head_dim ** -0.5).astype(jnp.bfloat16)
            k_rot = apply_rope(kv_proj[..., :head_dim].astype(jnp.float32), cos_tab, sin_tab).astype(jnp.bfloat16)
            v_val = kv_proj[..., head_dim:]
            scores = jnp.einsum("crie,cle->cirl", q_rot, k_rot, preferred_element_type=jnp.float32)
            scores = jnp.where(causal, scores, -1e30)
            attn_prob = jax.nn.softmax(scores, axis=-1).astype(jnp.bfloat16)
            attn_out = jnp.einsum("cirl,cle->crie", attn_prob, v_val, preferred_element_type=jnp.float32).astype(jnp.bfloat16).reshape(tok_z, q_loc)
            mlp_out = (jax.nn.silu(gate_val.astype(jnp.float32)) * up_val.astype(jnp.float32)).astype(jnp.bfloat16)
            joined = jnp.concatenate([attn_out, mlp_out], axis=1)
            part = jnp.dot(joined, w_o, preferred_element_type=jnp.float32).astype(jnp.bfloat16)
            update = lax.psum_scatter(part, tp, scatter_dimension=0, tiled=True)
            hidden = hidden + update
            kv_outs.append(jnp.stack([k_rot, v_val]))

        y_parts = hidden.reshape(tok_loc, n_dev, d_local).transpose(1, 0, 2)
        y_loc = lax.all_to_all(y_parts, every, 0, 0, tiled=True).reshape(n_batch, seq_len, d_local)
        kv = jnp.stack(kv_outs).reshape(n_layers, 2, batch_loc, n_z, n_tp, seq_local, head_dim)
        me = lax.axis_index("y") * n_col + lax.axis_index("col")
        kv = lax.dynamic_index_in_dim(kv, me, axis=4, keepdims=False)
        kv = lax.all_to_all(kv, "z", 3, 2, tiled=True)
        kv = kv.reshape(n_layers, 2, n_batch, seq_local, head_dim)
        return y_loc, kv

    return jax.shard_map(device_fn, mesh=mesh4, in_specs=(act_spec, P(None, every), w_spec, w_spec, P(None, "col", ("z", "y"))), out_specs=(act_spec, P(None, None, None, every, None)), check_vma=False)
```

time: 2660 us -> 869 us (0.33)
  waiting for transfers between devices: 1750 us -> 499 us
  other arithmetic: 283 us -> 35.2 us
  blocking collectives: 262 us -> 129 us
  matrix products: 229 us -> 109 us
  local copies, waits for them, and re-layouts: 112 us -> 38.9 us
  starting transfers between devices: 0.54 us -> 35.7 us
    psum x2 -> x0, waiting for transfers between devices: 1630 us -> none  [device_fn(): main_proj, kv_piece = lax.psum((part_main, part_kv), 'row')]
    psum x4 -> x0, blocking collectives: 262 us -> none  [the longest x2 137 us: device_fn(): lax.psum(jnp.sum(hidden_f32, axis=-1, keepdims=True), ('row', 'col'))]
    all_gather x4 -> x6, waiting for transfers between devices: 59 us -> 298 us  [the longest x2 150 us: device_fn(): h = lax.all_gather(normed, tp, axis=0, tiled=True)]
    sub x6 -> x0, other arithmetic: 168 us -> none  [the longest x2 132 us: device_fn(): attn_prob = jax.nn.softmax(scores, axis=-1).astype(jnp.bfloat16)]
    all_gather x0 -> x5, blocking collectives: none -> 110 us  [the longest x2 43.4 us: device_fn(): wkv = lax.all_gather(wkv, 'y', axis=0, tiled=True)]
    reduce_scatter x2, waiting for transfers between devices: 62.8 us -> 171 us  [device_fn(): update = lax.psum_scatter(part, tp, scatter_dimension=0, tiled=True)]
    dot_general x2, matrix products: 68.5 us -> 2.41 us  [device_fn(): jnp.einsum('crie,cle->cirl', q_rot, k_rot, preferred_element_type=jnp.flo...]
    convert_element_type x2, other arithmetic: 67.7 us -> 8.36 us  [device_fn(): (jax.nn.silu(gate_val.astype(jnp.float32)) * up_val.astype(jnp.float32))....]
  transfers between devices with their start and end apart: 8 -> 14, of which waited for: 6 -> 10; matrix products, arithmetic and copies ran while one was open for 8% -> 14% of each run, Pallas kernels for 0% -> 0%
where the time goes in v1:
time: 869 us; the launch traced here: 861 us
  waiting for transfers between devices  499 us (57%)
  blocking collectives  129 us (15%)
  matrix products  109 us (13%)
  local copies, waits for them, and re-layouts  38.9 us (4%)
  starting transfers between devices  35.7 us (4%)
  other arithmetic  35.2 us (4%)
  between operations  14.8 us (2%)
    reduce_scatter x2, waiting for transfers between devices, device_fn(): update = lax.psum_scatter(part, tp, scatter_dimension=0, tiled=True)  171 us
    all_gather x2, waiting for transfers between devices, device_fn(): h = lax.all_gather(normed, tp, axis=0, tiled=True)  150 us
    all_gather x2, waiting for transfers between devices, device_fn(): lax.all_gather(jnp.concatenate([wi, wkv], axis=1), 'z', axis=0, tiled=True)  121 us
    dot_general x2, matrix products, device_fn(): jnp.dot(h, w_i, preferred_element_type=jnp.float32).astype(jnp.bfloat16)  64.5 us
    all_gather x2, blocking collectives, device_fn(): wkv = lax.all_gather(wkv, 'y', axis=0, tiled=True)  43.4 us
    dot_general x2, matrix products, device_fn(): jnp.dot(joined, w_o, preferred_element_type=jnp.float32)  39.4 us
    all_gather x1, blocking collectives, device_fn(): gain = lax.all_gather(gain_loc, every, axis=1, tiled=True)  38.4 us
    all_gather x2, waiting for transfers between devices, device_fn(): wo = lax.all_gather(wo, 'z', axis=1, tiled=True)  28.2 us
  transfers between devices with their start and end apart: 14, of which 10 were waited for; matrix products, arithmetic and copies ran while one was open for 14% of the time, Pallas kernels for 0%

profile of v1, /device:TPU:1, one launch (start us, length us, event | category | flops | bytes accessed | tf_op | source)
XLA Modules:
  0.0 860.8 jit_solution(1311275958772600994)
XLA Ops:
  7.2 4.8 fusion.75
  12.0 2.8 copy.136
  15.0 1.6 maximum_bitcast_fusion
  16.6 5.0 all-to-all-start.1
  21.6 13.9 %all-gather = bf16[1,256,256]{1,2,0:T(8,128)(2,1)S(1)} all-gather(bf16[1,256,32]{1,2,0:T(8,128)(2,1)S(1)} %get-tuple-element.35), channel_id=2, replica_groups=mesh['z'=4,'y'=4,'col'=8] {'col'}, dimensions={2}, use_global_device_ids=true | all-gather | bytes 147456 | tf_op jit(solution)/shard_map/all_gather | solution.py:69
  35.6 22.0 %all-gather.1 = bf16[1,1024,256]{2,1,0:T(8,128)(2,1)S(1)} all-gather(bf16[1,256,256]{2,1,0:T(8,128)(2,1)S(1)} %copy.102), channel_id=3, replica_groups=mesh['z'=4,'y'=4,'col'=8] {'y'}, dimensions={1}, use_global_device_ids=true | all-gather | bytes 655360 | tf_op jit(solution)/shard_map/all_gather | solution.py:70
  57.6 2.5 copy.101
  60.1 3.5 pad_maximum_fusion
  65.2 1.4 reshape.437
  66.6 10.0 %all-to-all-start = ((bf16[128,2,1024]{2,1,0:T(2,128)(2,1)}), bf16[128,2,1024]{2,1,0:T(2,128)(2,1)S(1)}, u32[]{:S(2)}, u32[]{:S(2)}) async-start(bf16[128,2,1024]{2,1,0:T(2,128)(2,1)} %reshape.437), calls=%async_computation | async-start | bytes 1048576 | tf_op jit(solution)/shard_map/all_to_all | solution.py:79
  76.7 38.4 %all-gather.4 = bf16[128,32,2]{1,2,0:T(2,128)(2,1)S(1)} all-gather(bf16[1,32,2]{1,2,0:T(2,128)(2,1)S(1)} %bitcast.193), channel_id=1, replica_groups=mesh['z'=4,'y'=4,'col'=8] {'z','y','col'}, dimensions={0}, use_global_device_ids=true | all-gather | bytes 16512 | tf_op jit(solution)/shard_map/all_gather | solution.py:59
  119.5 2.6 fusion.77
  123.4 3.5 all-to-all-start.2
  128.1 16.4 %all-to-all-done.2 = bf16[4,640,256]{2,1,0:T(8,128)(2,1)S(1)} async-done(((bf16[4,640,256]{2,1,0:T(8,128)(2,1)}), bf16[4,640,256]{2,1,0:T(8,128)(2,1)S(1)}, u32[]{:S(2)}, u32[]{:S(2)}) %all-to-all-start.2) | async-done | bytes 1310752 | tf_op jit(solution)/shard_map/all_to_all | solution.py:74
  144.5 1.5 copy.106
  146.3 33.5 %all-gather.14.cloned.1.call-done = bf16[4096,1408]{1,0:T(8,128)(2,1)} async-done(((bf16[1024,1408]{1,0:T(8,128)(2,1)}), bf16[4096,1408]{1,0:T(8,128)(2,1)}) %all-gather.14.cloned.1.call-update) | async-done | bytes 11534352 | tf_op jit(solution)/shard_map/all_gather | solution.py:71
  179.8 73.2 %all-gather.12.cloned.1.call-done = bf16[2048,4096]{1,0:T(8,128)(2,1)} async-done(((bf16[64,4096]{1,0:T(8,128)(2,1)}), bf16[2048,4096]{1,0:T(8,128)(2,1)}) %all-gather.12.cloned.1.call-update) | async-done | bytes 16777232 | tf_op jit(solution)/shard_map/all_gather | solution.py:89
  252.9 32.2 %convolution_convert_fusion.3 = bf16[2048,1408]{1,0:T(8,128)(2,1)S(1)} fusion(bf16[2048,4096]{1,0:T(8,128)(2,1)} %all-gather.12.cloned.1.call-done, bf16[4096,1408]{1,0:T(8,128)(2,1)} %all-gather.14.cloned.1.call-done), kind=kOutput, calls=%fused_computation.3 | convolution fusion | flops 23625203712 | bytes 34078720 | tf_op jit(solution)/shard_map/dot_general | solution.py:90
  285.3 1.3 fusion.80
  290.3 1.3 fusion.39
  292.6 3.5 fusion.9
  296.1 14.5 %all-gather.16.cloned.1.call-done = bf16[640,4096]{0,1:T(8,128)(2,1)} async-done(((bf16[640,1024]{0,1:T(8,128)(2,1)}), bf16[640,4096]{0,1:T(8,128)(2,1)}) %all-gather.16.cloned.1.call-update) | async-done | bytes 5242896 | tf_op jit(solution)/shard_map/all_gather | solution.py:76
  310.6 19.7 %convolution_convert_fusion.1 = bf16[2048,4096]{1,0:T(8,128)(2,1)} fusion(bf16[640,4096]{0,1:T(8,128)(2,1)} %all-gather.16.cloned.1.call-done, bf16[2048,512]{1,0:T(8,128)(2,1)S(1)} %fusion.9, bf16[2048,128]{1,0:T(8,128)(2,1)} %bitcast.186), kind=kOutput, calls=%fused_computation.1 | convolution fusion | flops 10751049728 | bytes 24641536 | tf_op jit(solution)/shard_map/dot_general | solution.py:104
  330.3 2.8 copy.137
  333.3 1.6 maximum_bitcast_fusion.1
  334.9 4.0 all-to-all-start.3
  338.9 14.0 %all-gather.2 = bf16[1,256,256]{1,2,0:T(8,128)(2,1)} all-gather(bf16[1,256,32]{1,2,0:T(8,128)(2,1)S(1)} %get-tuple-element.34), channel_id=4, replica_groups=mesh['z'=4,'y'=4,'col'=8] {'col'}, dimensions={2}, use_global_device_ids=true | all-gather | bytes 147456 | tf_op jit(solution)/shard_map/all_gather | solution.py:69
  353.9 21.4 %all-gather.3 = bf16[1,1024,256]{2,1,0:T(8,128)(2,1)} all-gather(bf16[1,256,256]{2,1,0:T(8,128)(2,1)S(1)} %copy.110), channel_id=5, replica_groups=mesh['z'=4,'y'=4,'col'=8] {'y'}, dimensions={1}, use_global_device_ids=true | all-gather | bytes 655360 | tf_op jit(solution)/shard_map/all_gather | solution.py:70
  375.3 2.5 copy.109
  377.8 3.7 pad_maximum_fusion.1
  381.5 63.0 %reduce-scatter.3.cloned.1.call-done = bf16[64,4096]{1,0:T(8,128)(2,1)} async-done(((bf16[2048,4096]{1,0:T(8,128)(2,1)}), bf16[64,4096]{1,0:T(8,128)(2,1)}) %reduce-scatter.3.cloned.1.call-update) | async-done | bytes 524304 | tf_op jit(solution)/shard_map/reduce_scatter | solution.py:105
  444.5 1.3 convert_reduce_fusion.1
  447.2 1.3 pad_maximum_fusion.3
  448.5 18.9 %all_to_all.45 = bf16[4,640,256]{2,1,0:T(8,128)(2,1)} all-to-all(bf16[4,640,256]{2,1,0:T(8,128)(2,1)S(1)} %pad_maximum_fusion.3), channel_id=1, replica_groups=mesh['z'=4,'y'=4,'col'=8] {'y'}, dimensions={0} | all-to-all | bytes 2621440 | tf_op jit(solution)/shard_map/all_to_all | solution.py:74
  467.5 2.4 copy.114
  470.0 87.1 %all-gather.20.cloned.1.call-done = bf16[4096,1408]{1,0:T(8,128)(2,1)} async-done(((bf16[1024,1408]{1,0:T(8,128)(2,1)}), bf16[4096,1408]{1,0:T(8,128)(2,1)}) %all-gather.20.cloned.1.call-update) | async-done | bytes 11534352 | tf_op jit(solution)/shard_map/all_gather | solution.py:71
  557.0 76.6 %all-gather.18.cloned.1.call-done = bf16[2048,4096]{1,0:T(8,128)(2,1)} async-done(((bf16[64,4096]{1,0:T(8,128)(2,1)}), bf16[2048,4096]{1,0:T(8,128)(2,1)}) %all-gather.18.cloned.1.call-update) | async-done | bytes 16777232 | tf_op jit(solution)/shard_map/all_gather | solution.py:89
  633.6 32.3 %convolution_convert_fusion.2 = bf16[2048,1408]{1,0:T(8,128)(2,1)S(1)} fusion(bf16[2048,4096]{1,0:T(8,128)(2,1)} %all-gather.18.cloned.1.call-done, bf16[4096,1408]{1,0:T(8,128)(2,1)} %all-gather.20.cloned.1.call-done), kind=kOutput, calls=%fused_computation.2 | convolution fusion | flops 23625203712 | bytes 34078720 | tf_op jit(solution)/shard_map/dot_general | solution.py:90
  666.2 1.3 fusion.81
  671.1 1.3 fusion.36
  672.7 4.9 fusion.8
  677.5 13.7 %all-gather.22.cloned.1.call-done = bf16[640,4096]{0,1:T(8,128)(2,1)} async-done(((bf16[640,1024]{0,1:T(8,128)(2,1)}), bf16[640,4096]{0,1:T(8,128)(2,1)}) %all-gather.22.cloned.1.call-update) | async-done | bytes 5242896 | tf_op jit(solution)/shard_map/all_gather | solution.py:76
  691.2 19.7 %convolution_convert_fusion = bf16[2048,4096]{1,0:T(8,128)(2,1)} fusion(bf16[640,4096]{0,1:T(8,128)(2,1)} %all-gather.22.cloned.1.call-done, bf16[2048,512]{1,0:T(8,128)(2,1)} %fusion.8, bf16[2048,128]{1,0:T(8,128)(2,1)S(1)} %bitcast.187), kind=kOutput, calls=%fused_computation | convolution fusion | flops 10751049728 | bytes 24641536 | tf_op jit(solution)/shard_map/dot_general | solution.py:104
  713.9 3.3 all-to-all-start.6
  717.2 108.0 %reduce-scatter.5.cloned.1.call-done = bf16[64,4096]{1,0:T(8,128)(2,1)} async-done(((bf16[2048,4096]{1,0:T(8,128)(2,1)}), bf16[64,4096]{1,0:T(8,128)(2,1)}) %reduce-scatter.5.cloned.1.call-update) | async-done | bytes 524304 | tf_op jit(solution)/shard_map/reduce_scatter | solution.py:105
  826.9 1.4 reshape.439
  828.3 9.3 %all-to-all-start.5 = ((bf16[128,2,1024]{2,1,0:T(2,128)(2,1)}), bf16[128,2,1024]{2,1,0:T(2,128)(2,1)S(1)}, u32[]{:S(2)}, u32[]{:S(2)}) async-start(bf16[128,2,1024]{2,1,0:T(2,128)(2,1)} %reshape.439), calls=%async_computation.7 | async-start | bytes 1048576 | tf_op jit(solution)/shard_map/all_to_all | solution.py:110
  838.3 12.7 %all-to-all-done.5 = bf16[128,2,1024]{2,1,0:T(2,128)(2,1)S(1)} async-done(((bf16[128,2,1024]{2,1,0:T(2,128)(2,1)}), bf16[128,2,1024]{2,1,0:T(2,128)(2,1)S(1)}, u32[]{:S(2)}, u32[]{:S(2)}) %all-to-all-start.5) | async-done | bytes 524320 | tf_op jit(solution)/shard_map/all_to_all | solution.py:110
  (104 shorter events, 28.4 us)
Async XLA Ops:
  15.0 6.6 copy-start.12
  16.6 41.0 %all-to-all-start.1 = ((bf16[4,256,1152]{1,2,0:T(8,128)(2,1)}), bf16[4,256,1152]{1,2,0:T(8,128)(2,1)S(1)}, u32[]{:S(2)}, u32[]{:S(2)}) async-start(bf16[4,256,1152]{1,2,0:T(8,128)(2,1)} %maximum_bitcast_fusion), calls=%async_computation.1 | async-start | bytes 4718592 | tf_op jit(solution)/shard_map/all_to_all | solution.py:68
  21.6 158.2 %all-gather.14.cloned.1.call-start = ((), (), s32[]{:S(2)}) async-start(), calls=%async_computation.10 | async-start | bytes 14417920 | tf_op jit(solution)/shard_map/all_gather | solution.py:71
  60.1 3.5 copy-start.11
  63.6 13.0 %copy-start.13 = (bf16[2,32]{1,0:T(2,128)(2,1)S(1)}, bf16[2,32]{1,0:T(2,128)(2,1)}, u32[]{:S(2)}) copy-start(bf16[2,32]{1,0:T(2,128)(2,1)} %param.6) | copy-start | bytes 388
  66.6 48.7 %all-to-all-start = ((bf16[128,2,1024]{2,1,0:T(2,128)(2,1)}), bf16[128,2,1024]{2,1,0:T(2,128)(2,1)S(1)}, u32[]{:S(2)}, u32[]{:S(2)}) async-start(bf16[128,2,1024]{2,1,0:T(2,128)(2,1)} %reshape.437), calls=%async_computation | async-start | bytes 1048576 | tf_op jit(solution)/shard_map/all_to_all | solution.py:79
  76.6 176.3 %all-gather.12.cloned.1.call-start = ((), (), s32[]{:S(2)}) async-start(), calls=%async_computation.9 | async-start | bytes 17301504 | tf_op jit(solution)/shard_map/all_gather | solution.py:89
  116.2 5.9 copy-start.6
  123.4 21.1 %all-to-all-start.2 = ((bf16[4,640,256]{2,1,0:T(8,128)(2,1)}), bf16[4,640,256]{2,1,0:T(8,128)(2,1)S(1)}, u32[]{:S(2)}, u32[]{:S(2)}) async-start(bf16[4,640,256]{2,1,0:T(8,128)(2,1)} %pad_maximum_fusion.2), calls=%async_computation.2 | async-start | bytes 2621440 | tf_op jit(solution)/shard_map/all_to_all | solution.py:74
  126.9 183.7 %all-gather.16.cloned.1.call-start = ((), (), s32[]{:S(2)}) async-start(), calls=%async_computation.11 | async-start | bytes 6553600 | tf_op jit(solution)/shard_map/all_gather | solution.py:76
  146.0 298.5 %reduce-scatter.3.cloned.1.call-start = ((), (), s32[]{:S(2)}) async-start(), calls=%async_computation.12 | async-start | bytes 17301504 | tf_op jit(solution)/shard_map/reduce_scatter | solution.py:105
  285.1 2.6 copy-start.1
  287.8 1.7 copy-start.2
  287.8 1.7 copy-start.4
  334.9 40.4 %all-to-all-start.3 = ((bf16[4,256,1152]{1,2,0:T(8,128)(2,1)}), bf16[4,256,1152]{1,2,0:T(8,128)(2,1)S(1)}, u32[]{:S(2)}, u32[]{:S(2)}) async-start(bf16[4,256,1152]{1,2,0:T(8,128)(2,1)} %maximum_bitcast_fusion.1), calls=%async_computation.4 | async-start | bytes 4718592 | tf_op jit(solution)/shard_map/all_to_all | solution.py:68
  338.9 218.2 %all-gather.20.cloned.1.call-start = ((), (), s32[]{:S(2)}) async-start(), calls=%async_computation.14 | async-start | bytes 14417920 | tf_op jit(solution)/shard_map/all_gather | solution.py:71
  377.8 66.7 %copy-start.7 = (bf16[64,4096]{1,0:T(8,128)(2,1)S(1)}, bf16[64,4096]{1,0:T(8,128)(2,1)}, u32[]{:S(2)}) copy-start(bf16[64,4096]{1,0:T(8,128)(2,1)} %copy-done.6) | copy-start | bytes 1572868
  381.5 252.1 %all-gather.18.cloned.1.call-start = ((), (), s32[]{:S(2)}) async-start(), calls=%async_computation.13 | async-start | bytes 17301504 | tf_op jit(solution)/shard_map/all_gather | solution.py:89
  447.2 244.1 %all-gather.22.cloned.1.call-start = ((), (), s32[]{:S(2)}) async-start(), calls=%async_computation.15 | async-start | bytes 6553600 | tf_op jit(solution)/shard_map/all_gather | solution.py:76
  469.9 355.3 %reduce-scatter.5.cloned.1.call-start = ((), (), s32[]{:S(2)}) async-start(), calls=%async_computation.16 | async-start | bytes 17301504 | tf_op jit(solution)/shard_map/reduce_scatter | solution.py:105
  665.9 2.6 copy-start
  668.6 1.7 copy-start.8
  710.9 1.0 copy-start.3
  710.9 1.2 copy-start.5
  710.9 1.4 copy-start.9
  710.9 1.5 copy-start.10
  713.9 114.3 %all-to-all-start.6 = ((bf16[2,2,4,4,4,128]{5,4,2,1,0,3:T(4,128)(2,1)}), bf16[2,2,4,4,4,128]{5,4,2,1,0,3:T(4,128)(2,1)S(1)}, u32[]{:S(2)}, u32[]{:S(2)}) async-start(bf16[2,2,4,4,4,128]{5,4,2,1,0,3:T(4,128)(2,1)} %copy.123), calls=%async_computation.8 | async-start | bytes 131072 | tf_op jit(solution)/shard_map/all_to_all | solution.py:114
  828.3 22.8 %all-to-all-start.5 = ((bf16[128,2,1024]{2,1,0:T(2,128)(2,1)}), bf16[128,2,1024]{2,1,0:T(2,128)(2,1)S(1)}, u32[]{:S(2)}, u32[]{:S(2)}) async-start(bf16[128,2,1024]{2,1,0:T(2,128)(2,1)} %reshape.439), calls=%async_computation.7 | async-start | bytes 1048576 | tf_op jit(solution)/shard_map/all_to_all | solution.py:110
Sparse Core Ops, SparseCore 0:
  63.8 115.9 all-gather.13
  182.0 70.8 all-gather.11
  254.6 55.9 all-gather.15
  330.4 114.0 reduce-scatter.2
  446.0 110.9 all-gather.19
  559.7 73.8 all-gather.17
  635.3 55.9 all-gather.21
  711.1 114.0 reduce-scatter.4

commit v2 on v1

v2 whole, which is shorter than its diff:
```python
import functools

import jax
import jax.numpy as jnp
from jax import lax
from jax.experimental import pallas as pl
from jax.experimental.pallas import tpu as pltpu
from jax.sharding import Mesh
from jax.sharding import PartitionSpec as P

LN_EPS = 1e-6
RING = 4
CORES = 2
VMEM_LIMIT = 63 * 1024 * 1024


def rope_tables(positions, head_dim):
    half_dim = head_dim // 2
    inv_freq = 1.0 / (10000.0 ** (jnp.arange(half_dim, dtype=jnp.float32) * 2.0 / head_dim))
    angles = positions.astype(jnp.float32)[:, None] * inv_freq[None, :]
    return jnp.cos(angles), jnp.sin(angles)


def apply_rope(values, cos_tab, sin_tab):
    half_dim = values.shape[-1] // 2
    lower_half = values[..., :half_dim]
    upper_half = values[..., half_dim:]
    return jnp.concatenate([lower_half * cos_tab - upper_half * sin_tab, upper_half * cos_tab + lower_half * sin_tab], axis=-1)


def _place():
    return lax.axis_index("z"), lax.axis_index("y"), lax.axis_index("x"), lax.axis_index("core")


def _enter(me):
    z, y, x, c = me
    peers = [
        (z, lax.rem(y + 1, RING), x, c),
        (z, lax.rem(y + RING - 1, RING), x, c),
        (z, y, lax.rem(x + 1, RING), c),
        (z, y, lax.rem(x + RING - 1, RING), c),
        (z, y, x, 1 - c),
    ]
    sem = pltpu.get_barrier_semaphore()
    for dev in peers:
        pl.semaphore_signal(sem, inc=1, device_id=dev, device_id_type=pl.DeviceIdType.MESH)
    return len(peers)


def _enter_wait(count):
    pl.semaphore_wait(pltpu.get_barrier_semaphore(), count)


def ag_kernel(hid_ref, gain_ref, out_ref, h_ref, send_sem, recv_sem, dsend_sem, drecv_sem, loc_sem):
    me = _place()
    z, y, x, c = me
    n_peers = _enter(me)
    rows, d_model = hid_ref.shape
    quarter = rows // 4
    gain = gain_ref[...].astype(jnp.float32)
    for r in range(4):
        blk = hid_ref[r * quarter:(r + 1) * quarter, :].astype(jnp.float32)
        mean = jnp.mean(blk, axis=-1, keepdims=True)
        cen = blk - mean
        var = jnp.mean(cen * cen, axis=-1, keepdims=True)
        h_ref[r * quarter:(r + 1) * quarter, :] = (cen * lax.rsqrt(var + LN_EPS) * gain).astype(jnp.bfloat16)
    _enter_wait(n_peers)

    def shift(q, first, second):
        if q == 0:
            return lax.rem(y + second + RING, RING), lax.rem(x + first + RING, RING)
        return lax.rem(y + first + RING, RING), lax.rem(x + second + RING, RING)

    def span(q, part):
        if part is None:
            return pl.ds(q * 2 * quarter, 2 * quarter)
        return pl.ds((q * 2 + part) * quarter, quarter)

    offs = (0, -1, 1, 2)
    copies = {}

    def ici(idx, q, first, second, part, to_first, to_second, own=False):
        sy, sx = shift(q, first, second)
        ty, tx = shift(q, to_first, to_second)
        rws = span(q, part)
        dst = out_ref.at[sy, sx, c, rws]
        cp = pltpu.make_async_remote_copy(
            src_ref=h_ref.at[rws] if own else dst,
            dst_ref=dst,
            send_sem=send_sem.at[idx],
            recv_sem=recv_sem.at[idx],
            device_id=(z, ty, tx, c),
            device_id_type=pl.DeviceIdType.MESH,
        )
        cp.start()
        copies[idx] = cp

    dies = {}

    def die(idx, q, first, second, own=False):
        sy, sx = shift(q, first, second)
        rws = span(q, None)
        dst = out_ref.at[sy, sx, c, rws]
        cp = pltpu.make_async_remote_copy(
            src_ref=h_ref.at[rws] if own else dst,
            dst_ref=dst,
            send_sem=dsend_sem.at[idx],
            recv_sem=drecv_sem.at[idx],
            device_id=(z, y, x, 1 - c),
            device_id_type=pl.DeviceIdType.MESH,
        )
        cp.start()
        dies[idx] = cp

    def p1(q, d):
        return q * 20 + d

    def p1f(q, d):
        return q * 20 + 2 + d

    def p2(q, k, d):
        return q * 20 + 4 + k * 4 + d

    def p2f(q, k, d):
        return q * 20 + 4 + k * 4 + 2 + d

    sgn = (1, -1)
    for q in range(2):
        for d in range(2):
            ici(p1(q, d), q, 0, 0, None, sgn[d], 0, own=True)
    for q in range(2):
        for d in range(2):
            ici(p2(q, 0, d), q, 0, 0, None, 0, sgn[d], own=True)
    for q in range(2):
        die(q * 16, q, 0, 0, own=True)
    own = pltpu.make_async_copy(h_ref, out_ref.at[y, x, c], loc_sem)
    own.start()

    for d in range(2):
        for q in range(2):
            copies[p1(q, d)].wait_recv()
            src = -sgn[d]
            ici(p1f(q, d), q, src, 0, d, sgn[d], 0)
            for e in range(2):
                ici(p2(q, 1 + d, e), q, src, 0, None, 0, sgn[e])
            die(q * 16 + 1 + d, q, src, 0)
    for d in range(2):
        for q in range(2):
            copies[p2(q, 0, d)].wait_recv()
            src = -sgn[d]
            ici(p2f(q, 0, d), q, 0, src, d, 0, sgn[d])
            die(q * 16 + 4 + d, q, 0, src)
    for q in range(2):
        copies[p1f(q, 0)].wait_recv()
        copies[p1f(q, 1)].wait_recv()
        for e in range(2):
            ici(p2(q, 3, e), q, 2, 0, None, 0, sgn[e])
        die(q * 16 + 3, q, 2, 0)
    for k in (1, 2, 3):
        for d in range(2):
            for q in range(2):
                copies[p2(q, k, d)].wait_recv()
                src = -sgn[d]
                ici(p2f(q, k, d), q, offs[k], src, d, 0, sgn[d])
                die(q * 16 + 4 + k * 3 + d, q, offs[k], src)
    for k in range(4):
        for q in range(2):
            copies[p2f(q, k, 0)].wait_recv()
            copies[p2f(q, k, 1)].wait_recv()
            die(q * 16 + 4 + k * 3 + 2, q, offs[k], 2)
    for idx in sorted(dies):
        dies[idx].wait_recv()
    for idx in sorted(dies):
        dies[idx].wait_send()
    for idx in sorted(copies):
        copies[idx].wait_send()
    own.wait()


def all_gather_norm(hidden, gain, layer):
    rows, d_model = hidden.shape
    group = RING * RING * CORES
    out = pl.pallas_call(
        ag_kernel,
        out_shape=jax.ShapeDtypeStruct((RING, RING, CORES, rows, d_model), jnp.bfloat16),
        in_specs=[pl.BlockSpec(memory_space=pltpu.VMEM)] * 2,
        out_specs=pl.BlockSpec(memory_space=pl.ANY),
        scratch_shapes=[
            pltpu.VMEM((rows, d_model), jnp.bfloat16),
            pltpu.SemaphoreType.DMA((40,)),
            pltpu.SemaphoreType.DMA((40,)),
            pltpu.SemaphoreType.DMA((32,)),
            pltpu.SemaphoreType.DMA((32,)),
            pltpu.SemaphoreType.DMA,
        ],
        compiler_params=pltpu.CompilerParams(collective_id=2 * layer, has_side_effects=True),
        cost_estimate=pl.CostEstimate(flops=25_000_000_000, bytes_accessed=group * rows * d_model * 2, transcendentals=0),
        name=f"gather_norm_{layer}",
    )(hidden, gain)
    return out.reshape(group * rows, d_model)


SLOT_OFF = (2, 1, 3, 0)


def rs_kernel(join_ref, w_ref, hid_ref, out_ref, lhs, away, acc, die_in, in1, in2, in3, in4,
              dsend, drecv, send1, recv1, send2, recv2, send3, recv3, send4, recv4):
    me = _place()
    z, y, x, c = me
    n_peers = _enter(me)
    rows = join_ref.shape[3]
    half = w_ref.shape[1] // 2
    depth = w_ref.shape[0]
    for s in range(RING):
        for j in range(RING):
            yy = lax.rem(y + SLOT_OFF[s], RING)
            xx = lax.rem(x + SLOT_OFF[j], RING)
            for cc in range(CORES):
                val = join_ref[yy, xx, (1 - c) if cc == 0 else c]
                lhs[0, s, cc, j] = val
                lhs[1, j, cc, s] = val
    _enter_wait(n_peers)

    def peer(q, first, second):
        dy = first * (1 - q) + second * q
        dx = first * q + second * (1 - q)
        return (z, lax.rem(y + dy + RING, RING), lax.rem(x + dx + RING, RING), c)

    def remote(src, dst, ssem, rsem, dev):
        return pltpu.make_async_remote_copy(
            src_ref=src, dst_ref=dst, send_sem=ssem, recv_sem=rsem, device_id=dev, device_id_type=pl.DeviceIdType.MESH)

    def die_copy(q, s):
        return remote(away.at[q, s], die_in.at[q, s], dsend.at[q, s], drecv.at[q, s], (z, y, x, 1 - c))

    def first_copy(q, d):
        return remote(acc.at[q, 0, pl.ds(2 * d, 2)], in1.at[q, d], send1.at[q, d], recv1.at[q, d], peer(q, 1 - 2 * d, 0))

    def second_copy(q, d, h):
        return remote(acc.at[q, 1 + d, pl.ds(2 * h, 2)], in2.at[q, d, pl.ds(2 * h, 2)], send2.at[q, d, h], recv2.at[q, d, h], peer(q, 1 - 2 * d, 0))

    def third_copy(q, d):
        rws = pl.ds(d * (rows // 2), rows // 2)
        return remote(acc.at[q, 3, 0, rws], in3.at[q, d], send3.at[q, d], recv3.at[q, d], peer(q, 0, 1 - 2 * d))

    def fourth_copy(q, d):
        return remote(acc.at[q, 3, 1 + d], in4.at[q, d], send4.at[q, d], recv4.at[q, d], peer(q, 0, 1 - 2 * d))

    n_blk = min(half, 512)

    def tile(q, s):
        left = lhs[q, s].reshape(CORES * RING * rows, depth)

        @pl.loop(0, half // n_blk)
        def _(n):
            col = pl.multiple_of(n * n_blk, n_blk)
            wcol = pl.multiple_of(q * half + n * n_blk, n_blk)
            res = jnp.dot(left, w_ref[:, pl.ds(wcol, n_blk)], preferred_element_type=jnp.float32).astype(jnp.bfloat16)
            res = res.reshape(CORES, RING, rows, n_blk)
            away[q, s, :, :, pl.ds(col, n_blk)] = res[0]
            acc[q, s, :, :, pl.ds(col, n_blk)] = res[1]

    def pair_sum(q, s):
        die_copy(q, s).wait_recv()

        @pl.loop(0, RING)
        def _(j):
            acc[q, s, j] = acc[q, s, j] + die_in[q, s, j]

    @pl.loop(0, 2 * RING)
    def _(t):
        s = t // 2
        q = t % 2
        tile(q, s)
        die_copy(q, s).start()

        @pl.when(t >= 2)
        def _():
            pair_sum(q, s - 1)

        @pl.when(s == 1)
        def _():
            first_copy(q, 0).start()
            first_copy(q, 1).start()

        @pl.when(s == 2)
        def _():
            second_copy(q, 0, 1).start()

        @pl.when(s == 3)
        def _():
            second_copy(q, 1, 0).start()

    for q in range(2):
        pair_sum(q, 3)
    for q in range(2):
        first_copy(q, 0).wait_recv()
        for j in range(2):
            acc[q, 1, j] = acc[q, 1, j] + in1[q, 0, j]
        second_copy(q, 0, 0).start()
        first_copy(q, 1).wait_recv()
        for j in range(2):
            acc[q, 2, 2 + j] = acc[q, 2, 2 + j] + in1[q, 1, j]
        second_copy(q, 1, 1).start()

    def total(q, j):
        val = acc[q, 3, j].astype(jnp.float32) + in2[q, 0, j].astype(jnp.float32) + in2[q, 1, j].astype(jnp.float32)
        acc[q, 3, j] = val.astype(jnp.bfloat16)

    for h in (1, 0):
        pass
    for q in range(2):
        second_copy(q, 0, 1).wait_recv()
        second_copy(q, 1, 0).wait_recv()
    for q in range(2):
        second_copy(q, 0, 0).wait_recv()
        second_copy(q, 1, 1).wait_recv()
        total(q, 0)
        third_copy(q, 0).start()
        third_copy(q, 1).start()
        for j in (1, 2, 3):
            total(q, j)
    hrow = rows // 2
    for q in range(2):
        third_copy(q, 0).wait_recv()
        acc[q, 3, 1, pl.ds(0, hrow)] = acc[q, 3, 1, pl.ds(0, hrow)] + in3[q, 0]
        fourth_copy(q, 0).start()
        third_copy(q, 1).wait_recv()
        acc[q, 3, 2, pl.ds(hrow, hrow)] = acc[q, 3, 2, pl.ds(hrow, hrow)] + in3[q, 1]
        fourth_copy(q, 1).start()
    for q in range(2):
        fourth_copy(q, 0).wait_recv()
        fourth_copy(q, 1).wait_recv()
        cols = pl.ds(q * half, half)
        upd = acc[q, 3, 3].astype(jnp.float32) + in4[q, 0].astype(jnp.float32) + in4[q, 1].astype(jnp.float32)
        upd = upd.astype(jnp.bfloat16)
        out_ref[:, cols] = (hid_ref[:, cols].astype(jnp.float32) + upd.astype(jnp.float32)).astype(jnp.bfloat16)
    for q in range(2):
        for s in range(RING):
            die_copy(q, s).wait_send()
        for d in range(2):
            first_copy(q, d).wait_send()
            second_copy(q, d, 0).wait_send()
            second_copy(q, d, 1).wait_send()
            third_copy(q, d).wait_send()
            fourth_copy(q, d).wait_send()


def out_reduce_scatter(joined, w_out, hidden, layer):
    rows, d_model = hidden.shape
    depth = joined.shape[1]
    half = d_model // 2
    bf = jnp.bfloat16
    dma = pltpu.SemaphoreType.DMA
    return pl.pallas_call(
        rs_kernel,
        out_shape=jax.ShapeDtypeStruct((rows, d_model), bf),
        in_specs=[pl.BlockSpec(memory_space=pltpu.VMEM)] * 3,
        out_specs=pl.BlockSpec(memory_space=pltpu.VMEM),
        scratch_shapes=[
            pltpu.VMEM((2, RING, CORES, RING, rows, depth), bf),
            pltpu.VMEM((2, RING, RING, rows, half), bf),
            pltpu.VMEM((2, RING, RING, rows, half), bf),
            pltpu.VMEM((2, RING, RING, rows, half), bf),
            pltpu.VMEM((2, 2, 2, rows, half), bf),
            pltpu.VMEM((2, 2, RING, rows, half), bf),
            pltpu.VMEM((2, 2, rows // 2, half), bf),
            pltpu.VMEM((2, 2, rows, half), bf),
            dma((2, RING)), dma((2, RING)),
            dma((2, 2)), dma((2, 2)),
            dma((2, 2, 2)), dma((2, 2, 2)),
            dma((2, 2)), dma((2, 2)),
            dma((2, 2)), dma((2, 2)),
        ],
        compiler_params=pltpu.CompilerParams(collective_id=2 * layer + 1, has_side_effects=True, vmem_limit_bytes=VMEM_LIMIT),
        cost_estimate=pl.CostEstimate(flops=35_000_000_000, bytes_accessed=(joined.size + w_out.size) * 2, transcendentals=0),
        name=f"out_scatter_{layer}",
    )(joined.reshape(RING, RING, CORES, rows, depth), w_out, hidden)


def solution(mesh):
    row_size = mesh.shape["row"]
    n_col = mesh.shape["col"]
    n_z = row_size // RING
    n_y = RING
    n_x = n_col // CORES
    n_tp = n_y * n_col
    n_dev = row_size * n_col
    mesh4 = Mesh(mesh.devices.reshape(n_z, n_y, n_x, CORES), ("z", "y", "x", "core"))
    every = ("z", "y", "x", "core")
    tp = ("y", "x", "core")
    col = ("x", "core")
    act_spec = P(None, None, every)
    w_spec = P(None, ("z", "y"), col)

    def device_fn(x_loc, gain_loc, w_in_loc, w_kv_loc, w_out_loc):
        n_layers = w_in_loc.shape[0]
        n_batch, seq_len, d_local = x_loc.shape
        d_model = d_local * n_dev
        e_block = w_in_loc.shape[2]
        r_block = w_out_loc.shape[1]
        f_block = e_block - r_block
        q_block = r_block - f_block
        q_loc, f_loc = q_block // n_y, f_block // n_y
        head_dim = w_kv_loc.shape[2] * n_col // 2
        heads_local = q_loc // head_dim
        batch_loc = n_batch // n_z
        n_tok = n_batch * seq_len
        tok_z = n_tok // n_z
        tok_loc = n_tok // n_dev
        seq_local = seq_len // n_dev
        d_row = w_in_loc.shape[1]
        positions = jnp.arange(seq_len)
        cos_tab, sin_tab = rope_tables(positions, head_dim)
        causal = positions[None, :] <= positions[:, None]

        wkv = lax.all_gather(w_kv_loc, tp, axis=0, tiled=False)
        wkv = wkv.reshape(n_y, n_col, n_layers, d_row, -1).transpose(2, 0, 3, 1, 4).reshape(n_layers, n_y * d_row, 2 * head_dim)
        weights = []
        for l in range(n_layers):
            wi = w_in_loc[l]
            q_part = wi[:, :q_block].reshape(d_row, n_y, q_loc)
            g_part = wi[:, q_block:q_block + f_block].reshape(d_row, n_y, f_loc)
            u_part = wi[:, q_block + f_block:].reshape(d_row, n_y, f_loc)
            wi = jnp.concatenate([q_part, g_part, u_part], axis=2).transpose(1, 0, 2)
            wi = lax.all_to_all(wi, "y", 0, 0, tiled=True).reshape(n_y * d_row, q_loc + 2 * f_loc)
            wi = lax.all_gather(jnp.concatenate([wi, wkv[l]], axis=1), "z", axis=0, tiled=True)
            wo = w_out_loc[l]
            wo = jnp.concatenate([wo[:q_block].reshape(n_y, q_loc, -1), wo[q_block:].reshape(n_y, f_loc, -1)], axis=1)
            wo = lax.all_to_all(wo, "y", 0, 0, tiled=True)
            wo = wo.transpose(1, 0, 2).reshape(q_loc + f_loc, -1)
            wo = lax.all_gather(wo, "z", axis=1, tiled=True)
            weights.append((wi, wo))

        send = jnp.concatenate([
            x_loc.reshape(n_dev, tok_loc, d_local),
            jnp.broadcast_to(gain_loc[None], (n_dev, n_layers, d_local)),
        ], axis=1)
        got = lax.all_to_all(send, every, 0, 0, tiled=True)
        got = got.transpose(1, 0, 2).reshape(tok_loc + n_layers, d_model)
        hidden = got[:tok_loc]
        gain = got[tok_loc:]
        kv_outs = []
        for l in range(n_layers):
            w_i, w_o = weights[l]
            h = all_gather_norm(hidden, gain[l][None], l)
            proj = jnp.dot(h, w_i, preferred_element_type=jnp.float32).astype(jnp.bfloat16)
            query = proj[:, :q_loc].reshape(batch_loc, seq_len, heads_local, head_dim)
            gate_val = proj[:, q_loc:q_loc + f_loc]
            up_val = proj[:, q_loc + f_loc:q_loc + 2 * f_loc]
            kv_proj = proj[:, q_loc + 2 * f_loc:].reshape(batch_loc, seq_len, 2 * head_dim)
            q_rot = (apply_rope(query.astype(jnp.float32), cos_tab[:, None, :], sin_tab[:, None, :]) * head_dim ** -0.5).astype(jnp.bfloat16)
            k_rot = apply_rope(kv_proj[..., :head_dim].astype(jnp.float32), cos_tab, sin_tab).astype(jnp.bfloat16)
            v_val = kv_proj[..., head_dim:]
            scores = jnp.einsum("crie,cle->cirl", q_rot, k_rot, preferred_element_type=jnp.float32)
            scores = jnp.where(causal, scores, -1e30)
            attn_prob = jax.nn.softmax(scores, axis=-1).astype(jnp.bfloat16)
            attn_out = jnp.einsum("cirl,cle->crie", attn_prob, v_val, preferred_element_type=jnp.float32).astype(jnp.bfloat16).reshape(tok_z, q_loc)
            mlp_out = (jax.nn.silu(gate_val.astype(jnp.float32)) * up_val.astype(jnp.float32)).astype(jnp.bfloat16)
            joined = jnp.concatenate([attn_out, mlp_out], axis=1)
            hidden = out_reduce_scatter(joined, w_o, hidden, l)
            kv_outs.append(jnp.stack([k_rot, v_val]))

        y_parts = hidden.reshape(tok_loc, n_dev, d_local).transpose(1, 0, 2)
        y_loc = lax.all_to_all(y_parts, every, 0, 0, tiled=True).reshape(n_batch, seq_len, d_local)
        kv = jnp.stack(kv_outs).reshape(n_layers, 2, batch_loc, n_z, n_tp, seq_local, head_dim)
        me = (lax.axis_index("y") * n_x + lax.axis_index("x")) * CORES + lax.axis_index("core")
        kv = lax.dynamic_index_in_dim(kv, me, axis=4, keepdims=False)
        kv = lax.all_to_all(kv, "z", 3, 2, tiled=True)
        kv = kv.reshape(n_layers, 2, n_batch, seq_local, head_dim)
        return y_loc, kv

    return jax.shard_map(device_fn, mesh=mesh4, in_specs=(act_spec, P(None, every), w_spec, w_spec, P(None, col, ("z", "y"))), out_specs=(act_spec, P(None, None, None, every, None)), check_vma=False)
```

time: 869 us -> 543 us (0.62)
  waiting for transfers between devices: 499 us -> 35.3 us
  Pallas kernels: 0 us -> 235 us
  blocking collectives: 129 us -> 85.6 us
  matrix products: 109 us -> 70.2 us
  other arithmetic: 35.2 us -> 23.3 us
  starting transfers between devices: 35.7 us -> 25.9 us
    all_gather x4 -> x3, waiting for transfers between devices: 270 us -> 5.15 us  [the longest x1 5.11 us: device_fn(): wkv = lax.all_gather(w_kv_loc, tp, axis=0, tiled=False)]
    pallas_call x0 -> x4, Pallas kernels: none -> 235 us  [the longest x2 123 us: out_reduce_scatter(): pl.pallas_call(rs_kernel, out_shape=jax.ShapeDtypeStruct((rows, d_model),...]
    reduce_scatter x2 -> x0, waiting for transfers between devices: 171 us -> none  [device_fn(): update = lax.psum_scatter(part, tp, scatter_dimension=0, tiled=True)]
    all_gather x5 -> x0, blocking collectives: 110 us -> none  [the longest x2 43.4 us: device_fn(): wkv = lax.all_gather(wkv, 'y', axis=0, tiled=True)]
    all_to_all x0 -> x2, blocking collectives: none -> 65.2 us  [device_fn(): lax.all_to_all(wi, 'y', 0, 0, tiled=True)]
    dot_general x2 -> x0, matrix products: 39.4 us -> none  [device_fn(): jnp.dot(joined, w_o, preferred_element_type=jnp.float32)]
    all_gather x2, waiting for transfers between devices: 28.2 us -> 0.01 us  [device_fn(): wo = lax.all_gather(wo, 'z', axis=1, tiled=True)]
    all_to_all x3 -> x1, waiting for transfers between devices: 0.01 us -> 16.7 us  [device_fn(): got = lax.all_to_all(send, every, 0, 0, tiled=True)]
  transfers between devices with their start and end apart: 14 -> 9, of which waited for: 10 -> 3; matrix products, arithmetic and copies ran while one was open for 14% -> 24% of each run, Pallas kernels for 0% -> 44%
where the time goes in v2:
time: 543 us; the launch traced here: 534 us
  Pallas kernels  235 us (43%)
  blocking collectives  85.6 us (16%)
  matrix products  70.2 us (13%)
  local copies, waits for them, and re-layouts  44.8 us (8%)
  waiting for transfers between devices  35.3 us (7%)
  starting transfers between devices  25.9 us (5%)
  other arithmetic  23.3 us (4%)
  between operations  14.5 us (3%)
    pallas_call x2, Pallas kernels, out_reduce_scatter(): pl.pallas_call(rs_kernel, out_shape=jax.ShapeDtypeStruct((rows, d_model),...  123 us
    pallas_call x2, Pallas kernels, all_gather_norm(): pl.pallas_call(ag_kernel, out_shape=jax.ShapeDtypeStruct((RING, RING, COR...  112 us
    all_to_all x2, blocking collectives, device_fn(): lax.all_to_all(wi, 'y', 0, 0, tiled=True)  65.2 us
    dot_general x2, matrix products, device_fn(): jnp.dot(h, w_i, preferred_element_type=jnp.float32).astype(jnp.bfloat16)  64.4 us
    all_to_all x1, blocking collectives, device_fn(): wo = lax.all_to_all(wo, 'y', 0, 0, tiled=True)  20.4 us
    all_to_all x1, waiting for transfers between devices, device_fn(): got = lax.all_to_all(send, every, 0, 0, tiled=True)  16.7 us
    all_to_all x1, waiting for transfers between devices, device_fn(): lax.all_to_all(y_parts, every, 0, 0, tiled=True)  12.7 us
    unnamed x32, local copies, waits for them, and re-layouts  11.1 us
  transfers between devices with their start and end apart: 9, of which 3 were waited for; matrix products, arithmetic and copies ran while one was open for 24% of the time, Pallas kernels for 44%

profile of v2, /device:TPU:1, one launch (start us, length us, event | category | flops | bytes accessed | tf_op | source)
XLA Modules:
  0.0 534.0 jit_solution(13128651997519810106)
XLA Ops:
  7.9 4.8 fusion.60
  12.8 2.8 copy.122
  15.9 34.5 %all_to_all.45 = bf16[4,256,1152]{1,2,0:T(8,128)(2,1)} all-to-all(bf16[4,256,1152]{1,2,0:T(8,128)(2,1)S(1)} %maximum_bitcast_fusion), channel_id=1, replica_groups=mesh['z'=4,'y'=4,'x'=4,'core'=2] {'y'}, dimensions={0} | all-to-all | bytes 4718592 | tf_op jit(solution)/shard_map/all_to_all | solution.py:426
  50.4 3.0 copy.86
  53.4 5.1 all-gather.15.cloned.1.call-done
  58.5 2.1 copy.130
  61.2 1.0 copy.88
  62.2 2.8 pad_maximum_fusion
  65.1 1.9 fusion.61
  67.0 1.2 fusion.62
  68.2 20.4 %all_to_all.46 = bf16[4,640,256]{2,1,0:T(8,128)(2,1)S(1)} all-to-all(bf16[4,640,256]{2,1,0:T(8,128)(2,1)S(1)} %pad_maximum_fusion.4), channel_id=1, replica_groups=mesh['z'=4,'y'=4,'x'=4,'core'=2] {'y'}, dimensions={0} | all-to-all | bytes 2621440 | tf_op jit(solution)/shard_map/all_to_all | solution.py:430
  88.6 1.3 copy.125
  90.0 2.8 copy.123
  93.1 30.7 %all_to_all.47 = bf16[4,256,1152]{1,2,0:T(8,128)(2,1)} all-to-all(bf16[4,256,1152]{1,2,0:T(8,128)(2,1)S(1)} %maximum_bitcast_fusion.1), channel_id=1, replica_groups=mesh['z'=4,'y'=4,'x'=4,'core'=2] {'y'}, dimensions={0} | all-to-all | bytes 4718592 | tf_op jit(solution)/shard_map/all_to_all | solution.py:426
  123.9 3.0 copy.95
  127.2 1.8 pad_maximum_fusion.1
  130.7 1.6 copy.83
  132.3 9.2 %all-to-all-start = ((bf16[128,66,32]{1,2,0:T(8,128)(2,1)}), bf16[128,66,32]{1,2,0:T(8,128)(2,1)S(1)}, u32[]{:S(2)}, u32[]{:S(2)}) async-start(bf16[128,66,32]{1,2,0:T(8,128)(2,1)} %copy.83), calls=%async_computation | async-start | bytes 2097152 | tf_op jit(solution)/shard_map/all_to_all | solution.py:439
  141.7 1.2 pad_maximum_fusion.5
  142.8 1.0 multiply_cosine_fusion
  143.8 16.7 %all-to-all-done = bf16[128,66,32]{1,2,0:T(8,128)(2,1)S(1)} async-done(((bf16[128,66,32]{1,2,0:T(8,128)(2,1)}), bf16[128,66,32]{1,2,0:T(8,128)(2,1)S(1)}, u32[]{:S(2)}, u32[]{:S(2)}) %all-to-all-start) | async-done | bytes 540704 | tf_op jit(solution)/shard_map/all_to_all | solution.py:439
  160.5 3.5 all-to-all-start.4
  164.4 1.1 copy.84.hid_ref
  165.5 1.7 slice_reduce_fusion
  167.9 59.4 %gather_norm_0.1 = bf16[4,4,2,64,4096]{4,3,2,1,0:T(8,128)(2,1)} custom-call(bf16[64,4096]{1,0:T(8,128)(2,1)} %copy.84.hid_ref, bf16[1,4096]{1,0:T(2,128)(2,1)} %slice.139.gain_ref), custom_call_target="tpu_custom_call" | custom-call | flops 24999999488 | bytes 16777216 | tf_op jit(solution)/shard_map/gather_norm_0/pallas_call | solution.py:183
  228.0 1.3 copy.126
  229.3 32.2 %convolution_convert_fusion.1 = bf16[2048,1408]{1,0:T(8,128)(2,1)S(1)} fusion(bf16[2048,4096]{1,0:T(8,128)(2,1)} %bitcast.196, bf16[4096,1408]{1,0:T(8,128)(2,1)} %all-gather.7.cloned.1.call-done), kind=kOutput, calls=%fused_computation.1 | convolution fusion | flops 23625203712 | bytes 34078720 | tf_op jit(solution)/shard_map/dot_general | solution.py:447
  261.7 1.3 fusion.9
  264.9 1.2 fusion.10
  267.0 2.1 fusion.29
  269.1 2.1 copy.91
  271.1 3.0 pad_maximum_fusion.2.join_ref
  274.1 60.8 %out_scatter_0.1.hid_ref = bf16[64,4096]{1,0:T(8,128)(2,1)} custom-call(bf16[4,4,2,64,640]{4,3,2,1,0:T(8,128)(2,1)} %pad_maximum_fusion.2.join_ref, bf16[640,4096]{1,0:T(8,128)(2,1)} %all-gather.9.cloned.1.call-done.w_ref, bf16[64,4096]{1,0:T(8,128)(2,1)} %copy.84.hid_ref), custom_call_target="tpu_custom_call" | custom-call | flops 35000000512 | bytes 7864320 | tf_op jit(solution)/shard_map/out_scatter_0/pallas_call | solution.py:355
  334.9 52.1 %gather_norm_1.1 = bf16[4,4,2,64,4096]{4,3,2,1,0:T(8,128)(2,1)} custom-call(bf16[64,4096]{1,0:T(8,128)(2,1)} %out_scatter_0.1.hid_ref, bf16[1,4096]{1,0:T(2,128)(2,1)} %slice.158.gain_ref), custom_call_target="tpu_custom_call" | custom-call | flops 24999999488 | bytes 16777216 | tf_op jit(solution)/shard_map/gather_norm_1/pallas_call | solution.py:183
  387.1 32.2 %convolution_convert_fusion = bf16[2048,1408]{1,0:T(8,128)(2,1)S(1)} fusion(bf16[2048,4096]{1,0:T(8,128)(2,1)} %bitcast.197, bf16[4096,1408]{1,0:T(8,128)(2,1)} %all-gather.11.cloned.1.call-done), kind=kOutput, calls=%fused_computation | convolution fusion | flops 23625203712 | bytes 34078720 | tf_op jit(solution)/shard_map/dot_general | solution.py:447
  420.8 1.1 copy-done
  422.7 3.5 all-to-all-start.6
  426.1 1.1 convert.27
  427.8 1.2 fusion.11
  429.7 1.3 fusion.26
  431.3 3.5 fusion.8
  434.8 1.9 pad_maximum_fusion.3.join_ref
  436.7 62.2 %out_scatter_1.1 = bf16[64,4096]{1,0:T(8,128)(2,1)} custom-call(bf16[4,4,2,64,640]{4,3,2,1,0:T(8,128)(2,1)} %pad_maximum_fusion.3.join_ref, bf16[640,4096]{1,0:T(8,128)(2,1)} %all-gather.13.cloned.1.call-done.w_ref, bf16[64,4096]{1,0:T(8,128)(2,1)} %out_scatter_0.1.hid_ref), custom_call_target="tpu_custom_call" | custom-call | flops 35000000512 | bytes 7864320 | tf_op jit(solution)/shard_map/out_scatter_1/pallas_call | solution.py:355
  499.0 1.5 copy.101
  500.5 1.4 reshape.425
  501.9 9.3 %all-to-all-start.5 = ((bf16[128,2,1024]{2,1,0:T(2,128)(2,1)}), bf16[128,2,1024]{2,1,0:T(2,128)(2,1)S(1)}, u32[]{:S(2)}, u32[]{:S(2)}) async-start(bf16[128,2,1024]{2,1,0:T(2,128)(2,1)} %reshape.425), calls=%async_computation.5 | async-start | bytes 1048576 | tf_op jit(solution)/shard_map/all_to_all | solution.py:465
  511.8 12.7 %all-to-all-done.5 = bf16[128,2,1024]{2,1,0:T(2,128)(2,1)S(1)} async-done(((bf16[128,2,1024]{2,1,0:T(2,128)(2,1)}), bf16[128,2,1024]{2,1,0:T(2,128)(2,1)S(1)}, u32[]{:S(2)}, u32[]{:S(2)}) %all-to-all-start.5) | async-done | bytes 524320 | tf_op jit(solution)/shard_map/all_to_all | solution.py:465
  526.2 1.1 copy.111
  (79 shorter events, 14.8 us)
Async XLA Ops:
  7.2 51.4 %all-gather.15.cloned.1.call-start = ((), (), s32[]{:S(2)}) async-start(), calls=%async_computation.11 | async-start | bytes 1081344 | tf_op jit(solution)/shard_map/all_gather | solution.py:417
  7.9 221.4 %all-gather.7.cloned.1.call-start = ((), (), s32[]{:S(2)}) async-start(), calls=%async_computation.7 | async-start | bytes 14417920 | tf_op jit(solution)/shard_map/all_gather | solution.py:427
  65.0 2.0 copy-start.6
  65.0 209.1 %all-gather.9.cloned.1.call-start = ((), (), s32[]{:S(2)}) async-start(), calls=%async_computation.8 | async-start | bytes 6553600 | tf_op jit(solution)/shard_map/all_gather | solution.py:432
  89.9 297.1 %all-gather.11.cloned.1.call-start = ((), (), s32[]{:S(2)}) async-start(), calls=%async_computation.9 | async-start | bytes 14417920 | tf_op jit(solution)/shard_map/all_gather | solution.py:427
  127.2 1.8 copy-start.9
  129.0 0.9 copy-start.10
  129.9 11.7 %copy-start.5 = (bf16[1,2048,256]{2,1,0:T(8,128)(2,1)S(1)}, bf16[1,2048,256]{2,1,0:T(8,128)(2,1)}, u32[]{:S(2)}) copy-start(bf16[1,2048,256]{2,1,0:T(8,128)(2,1)} %get-tuple-element.14) | copy-start | bytes 3145732
  130.0 11.7 %copy-start.8 = (bf16[1,512,256]{2,1,0:T(8,128)(2,1)S(1)}, bf16[1,512,256]{2,1,0:T(8,128)(2,1)}, u32[]{:S(2)}) copy-start(bf16[1,512,256]{2,1,0:T(8,128)(2,1)} %get-tuple-element.12) | copy-start | bytes 786436
  132.3 28.2 %all-to-all-start = ((bf16[128,66,32]{1,2,0:T(8,128)(2,1)}), bf16[128,66,32]{1,2,0:T(8,128)(2,1)S(1)}, u32[]{:S(2)}, u32[]{:S(2)}) async-start(bf16[128,66,32]{1,2,0:T(8,128)(2,1)} %copy.83), calls=%async_computation | async-start | bytes 2097152 | tf_op jit(solution)/shard_map/all_to_all | solution.py:439
  160.5 67.5 %all-to-all-start.4 = ((bf16[4,640,256]{2,1,0:T(8,128)(2,1)}), bf16[4,640,256]{2,1,0:T(8,128)(2,1)S(1)}, u32[]{:S(2)}, u32[]{:S(2)}) async-start(bf16[4,640,256]{2,1,0:T(8,128)(2,1)} %pad_maximum_fusion.5), calls=%async_computation.4 | async-start | bytes 2621440 | tf_op jit(solution)/shard_map/all_to_all | solution.py:430
  164.1 272.6 %all-gather.13.cloned.1.call-start = ((), (), s32[]{:S(2)}) async-start(), calls=%async_computation.10 | async-start | bytes 6553600 | tf_op jit(solution)/shard_map/all_gather | solution.py:432
  264.4 1.7 copy-start.1
  264.4 1.7 copy-start.3
  419.3 2.7 copy-start
  419.3 2.6 copy-start.2
  419.4 2.6 copy-start.4
  419.4 2.6 copy-start.7
  422.7 79.2 %all-to-all-start.6 = ((bf16[2,2,4,4,4,128]{5,4,2,1,0,3:T(4,128)(2,1)}), bf16[2,2,4,4,4,128]{5,4,2,1,0,3:T(4,128)(2,1)S(1)}, u32[]{:S(2)}, u32[]{:S(2)}) async-start(bf16[2,2,4,4,4,128]{5,4,2,1,0,3:T(4,128)(2,1)} %copy.109), calls=%async_computation.6 | async-start | bytes 131072 | tf_op jit(solution)/shard_map/all_to_all | solution.py:469
  501.9 22.7 %all-to-all-start.5 = ((bf16[128,2,1024]{2,1,0:T(2,128)(2,1)}), bf16[128,2,1024]{2,1,0:T(2,128)(2,1)S(1)}, u32[]{:S(2)}, u32[]{:S(2)}) async-start(bf16[128,2,1024]{2,1,0:T(2,128)(2,1)} %reshape.425), calls=%async_computation.5 | async-start | bytes 1048576 | tf_op jit(solution)/shard_map/all_to_all | solution.py:465
Sparse Core Ops, SparseCore 0:
  10.2 48.2 all-gather.14
  65.1 118.4 all-gather.6
  185.3 58.5 all-gather.8
  245.3 110.5 all-gather.10
  357.5 58.0 all-gather.12

commit v3 on v0

v3 whole, which is shorter than its diff:
```python
import jax
import jax.numpy as jnp
from jax import lax
from jax.experimental import pallas as pl
from jax.experimental.pallas import tpu as pltpu
from jax.sharding import Mesh
from jax.sharding import PartitionSpec as P

LN_EPS = 1e-6
RING = 4
CORES = 2
VMEM_LIMIT = 67_000_000
BF = jnp.bfloat16
F32 = jnp.float32
SLOT_OFF = (2, 1, 3, 0)
SIGN = (1, -1)
NAMES = (
    "hid_in", "gain", "wkv", "w_in", "w_out", "cos", "sin", "hid_out", "kv_out", "h_all", "wi", "wo", "kvh", "h_ref",
    "wv", "kvb", "wov", "hb", "joined", "qkv", "stage", "lhs", "away", "acc", "die_in", "in1", "in2", "in3", "in4",
    "ag_send", "ag_recv", "ag_dsend", "ag_drecv", "ag_loc", "h_sem", "kvo_sem", "w_load", "y_recv", "zb_recv",
    "zc_recv", "w_send", "kz_send", "kz_recv", "ky_send", "ky_recv", "kx_send", "kx_recv", "kd_send", "kd_recv",
    "k_loc", "dsend", "drecv", "send1", "recv1", "send2", "recv2", "send3", "recv3", "send4", "recv4",
)


class Refs:
    def __init__(self, refs):
        for name, ref in zip(NAMES, refs, strict=True):
            setattr(self, name, ref)


def model_kernel(*refs):
    r = Refs(refs)
    z, y, x, c = (lax.axis_index(a) for a in ("z", "y", "x", "core"))
    n_layers = r.gain.shape[0]
    rows, d_model = r.hid_in.shape
    seq_len, head_dim = r.cos.shape
    d_row = r.w_in.shape[1]
    e_loc = r.wi.shape[3]
    depth = r.wo.shape[3]
    f_loc = depth - head_dim
    quarter = rows // 4
    half = d_model // 2
    q_block = head_dim * RING
    f_block = f_loc * RING

    def turn(base, off):
        return lax.rem(base + off + RING, RING)

    def remote(src, dst, ssem, rsem, dev):
        return pltpu.make_async_remote_copy(
            src_ref=src, dst_ref=dst, send_sem=ssem, recv_sem=rsem, device_id=dev, device_id_type=pl.DeviceIdType.MESH)

    partner = (z, y, x, 1 - c)

    peers = [(turn(z, o), y, x, c) for o in (1, 2, 3)]
    peers += [(z, turn(y, o), x, c) for o in (1, 2, 3)]
    peers += [(z, y, turn(x, o), c) for o in (1, 2, 3)]
    peers.append(partner)
    gate_sem = pltpu.get_barrier_semaphore()
    for dev in peers:
        pl.semaphore_signal(gate_sem, inc=1, device_id=dev, device_id_type=pl.DeviceIdType.MESH)
    pl.semaphore_wait(gate_sem, len(peers))

    def hook(pump, i):
        with jax.named_scope(f"hook_{i}"):
            pump(i)

    def w_cols(kind):
        return pl.ds(0, head_dim + f_loc) if kind == 0 else pl.ds(head_dim + f_loc, f_loc)

    def piece(t, zz, yy):
        l, kind = t // 3, t % 3
        if kind == 2:
            return r.wo.at[l, zz, yy]
        return r.wi.at[l, zz, pl.ds(pl.multiple_of(yy * d_row, d_row), d_row), w_cols(kind)]

    def piece_half(t, zz, yy, h):
        l, kind = t // 3, t % 3
        if kind == 2:
            return r.wo.at[l, zz, yy, pl.ds(h * (depth // 2), depth // 2)]
        return r.wi.at[l, zz, pl.ds(pl.multiple_of(yy * d_row + h * (d_row // 2), d_row // 2), d_row // 2), w_cols(kind)]

    def own_parts(t, owner, zz, yy):
        l, kind = t // 3, t % 3
        hq = pl.ds(pl.multiple_of(owner * head_dim, head_dim), head_dim)
        if kind == 2:
            return [
                (r.w_out.at[l, hq], r.wo.at[l, zz, yy, pl.ds(0, head_dim)]),
                (r.w_out.at[l, pl.ds(pl.multiple_of(q_block + owner * f_loc, head_dim), f_loc)], r.wo.at[l, zz, yy, pl.ds(head_dim, f_loc)]),
            ]
        rws = pl.ds(pl.multiple_of(yy * d_row, d_row), d_row)
        if kind == 0:
            return [
                (r.w_in.at[l, :, hq], r.wi.at[l, zz, rws, pl.ds(0, head_dim)]),
                (r.w_in.at[l, :, pl.ds(pl.multiple_of(q_block + owner * f_loc, head_dim), f_loc)], r.wi.at[l, zz, rws, pl.ds(head_dim, f_loc)]),
            ]
        return [(r.w_in.at[l, :, pl.ds(pl.multiple_of(q_block + f_block + owner * f_loc, head_dim), f_loc)],
                 r.wi.at[l, zz, rws, pl.ds(head_dim + f_loc, f_loc)])]

    def y_send(t):
        for dy in (1, 3, 2):
            owner = turn(y, dy)
            for src, dst in own_parts(t, owner, z, y):
                remote(src, dst, r.w_send.at[t, 0], r.y_recv.at[t, (RING - dy) % RING], (z, owner, x, c)).start()

    def z_own(t):
        for d in range(2):
            for src, dst in own_parts(t, y, z, y):
                remote(src, dst, r.w_send.at[t, 1], r.zb_recv.at[t, 0, d], (turn(z, SIGN[d]), y, x, c)).start()

    def z_direct(t, j):
        yy = turn(y, j)
        ref = piece(t, z, yy)
        remote(ref, ref, r.w_send.at[t, 0], r.y_recv.at[t, j], (z, y, x, c)).wait_recv()
        for d in range(2):
            remote(ref, ref, r.w_send.at[t, 1], r.zb_recv.at[t, j, d], (turn(z, SIGN[d]), y, x, c)).start()

    def z_forward(t, j):
        yy = turn(y, j)
        for d in range(2):
            zz = turn(z, -SIGN[d])
            ref = piece(t, zz, yy)
            remote(ref, ref, r.w_send.at[t, 1], r.zb_recv.at[t, j, d], (z, y, x, c)).wait_recv()
            part = piece_half(t, zz, yy, d)
            remote(part, part, r.w_send.at[t, 2], r.zc_recv.at[t, j, d], (turn(z, SIGN[d]), y, x, c)).start()

    def place(t, zz):
        l, kind = t // 3, t % 3
        if kind == 2:
            return r.wo.at[l, zz], r.wov.at[zz]
        return r.wi.at[l, zz, :, w_cols(kind)], r.wv.at[zz, :, w_cols(kind)]

    def load_near(t):
        l, kind = t // 3, t % 3
        for d in range(2):
            src, dst = place(t, turn(z, SIGN[d]))
            pltpu.make_async_copy(src, dst, r.w_load.at[kind]).start()
        for j in (1, 2, 3):
            yy = turn(y, j)
            dst = r.wov.at[z, yy] if kind == 2 else r.wv.at[z, pl.ds(pl.multiple_of(yy * d_row, d_row), d_row), w_cols(kind)]
            pltpu.make_async_copy(piece(t, z, yy), dst, r.w_load.at[kind]).start()
        for src, dst in own_parts(t, y, z, y):
            if kind == 2:
                pass
            pltpu.make_async_copy(src, own_place(t, dst, src), r.w_load.at[kind]).start()

    def own_place(t, dst, src):
        kind = t % 3
        if kind == 2:
            n = src.shape[0]
            return r.wov.at[z, y, pl.ds(0 if n == head_dim and f_loc != head_dim else head_dim, n)]
        n = src.shape[1]
        rws = pl.ds(pl.multiple_of(y * d_row, d_row), d_row)
        if kind == 0:
            return r.wv.at[z, rws, pl.ds(0 if n == head_dim and f_loc != head_dim else head_dim, n)]
        return r.wv.at[z, rws, pl.ds(head_dim + f_loc, f_loc)]

    def finish(t):
        l, kind = t // 3, t % 3
        far = turn(z, 2)
        for j in range(RING):
            for d in range(2):
                part = piece_half(t, far, turn(y, j), d)
                remote(part, part, r.w_send.at[t, 2], r.zc_recv.at[t, j, d], (z, y, x, c)).wait_recv()
        load_near(t)
        src, dst = place(t, far)
        pltpu.make_async_copy(src, dst, r.w_load.at[kind]).start()

    def loaded(t):
        kind = t % 3
        dst = r.wov if kind == 2 else r.wv.at[:, :, w_cols(kind)]
        pltpu.make_async_copy(dst, dst, r.w_load.at[kind]).wait()

    def drain(t):
        l, kind = t // 3, t % 3
        if kind == 2:
            refs3 = (r.wo.at[l, 0, pl.ds(0, 3)], r.wo.at[l, pl.ds(0, 2)], r.wo.at[l, 0])
        else:
            cols = w_cols(kind)
            refs3 = (r.wi.at[l, 0, pl.ds(0, 3 * d_row), cols], r.wi.at[l, pl.ds(0, 2), :, cols], r.wi.at[l, 0, :, cols])
        for g in range(3):
            remote(refs3[g], refs3[g], r.w_send.at[t, g], r.y_recv.at[t, 0], (z, y, x, c)).wait_send()

    def kv_z():
        for i, o in enumerate((1, 3, 2)):
            remote(r.wkv, r.kvh.at[x, c, :, y, z], r.kz_send.at[i], r.kz_recv.at[i], (turn(z, o), y, x, c)).start()
        pltpu.make_async_copy(r.wkv, r.kvh.at[x, c, :, y, z], r.k_loc.at[0]).start()

    def kv_y():
        pltpu.make_async_copy(r.wkv, r.kvh.at[x, c, :, y, z], r.k_loc.at[0]).wait()
        for i, o in enumerate((1, 3, 2)):
            zz = turn(z, -o)
            remote(r.wkv, r.kvh.at[x, c, :, y, zz], r.kz_send.at[i], r.kz_recv.at[i], (turn(z, o), y, x, c)).wait()
        ref = r.kvh.at[x, c, :, y]
        for i, o in enumerate((1, 3, 2)):
            remote(ref, ref, r.ky_send.at[i], r.ky_recv.at[i], (z, turn(y, o), x, c)).start()

    def kv_x():
        for i, o in enumerate((1, 3, 2)):
            ref = r.kvh.at[x, c, :, turn(y, -o)]
            remote(ref, ref, r.ky_send.at[i], r.ky_recv.at[i], (z, turn(y, o), x, c)).wait()
        for l in range(n_layers):
            ref = r.kvh.at[x, c, l]
            for i, o in enumerate((1, 3, 2)):
                remote(ref, ref, r.kx_send.at[l, i], r.kx_recv.at[l, i], (z, y, turn(x, o), c)).start()
            remote(ref, ref, r.kd_send.at[l, 3], r.kd_recv.at[l, 3], partner).start()

    def kv_die(l):
        for i, o in enumerate((1, 3, 2)):
            ref = r.kvh.at[turn(x, -o), c, l]
            remote(ref, ref, r.kx_send.at[l, i], r.kx_recv.at[l, i], (z, y, turn(x, o), c)).wait()
            remote(ref, ref, r.kd_send.at[l, i], r.kd_recv.at[l, i], partner).start()

    def kv_load(l):
        for i, o in enumerate((1, 3, 2, 0)):
            ref = r.kvh.at[turn(x, -o), 1 - c, l]
            remote(ref, ref, r.kd_send.at[l, i], r.kd_recv.at[l, i], partner).wait()
        kc = r.wkv.shape[1]
        for xx in range(RING):
            for cc in range(CORES):
                pltpu.make_async_copy(r.kvh.at[xx, cc, l], r.kvb.at[:, :, pl.ds((xx * CORES + cc) * kc, kc)], r.k_loc.at[1]).start()

    def kv_loaded():
        pltpu.make_async_copy(r.kvb, r.kvb, r.k_loc.at[1]).wait()

    def gather_norm(l, pump):
        hid = r.hid_in if l == 0 else r.hid_out
        gain = r.gain[l:l + 1, :].astype(F32)
        for b in range(4):
            blk = hid[b * quarter:(b + 1) * quarter, :].astype(F32)
            mean = jnp.mean(blk, axis=-1, keepdims=True)
            cen = blk - mean
            var = jnp.mean(cen * cen, axis=-1, keepdims=True)
            r.h_ref[b * quarter:(b + 1) * quarter, :] = (cen * lax.rsqrt(var + LN_EPS) * gain).astype(BF)
        out = r.h_all.at[l]

        def spot(q, first, second):
            if q == 0:
                return turn(y, second), turn(x, first)
            return turn(y, first), turn(x, second)

        def span(q, part):
            if part is None:
                return pl.ds(q * 2 * quarter, 2 * quarter)
            return pl.ds((q * 2 + part) * quarter, quarter)

        copies = {}

        def ici(idx, grp, q, first, second, part, to_first, to_second, own=False):
            sy, sx = spot(q, first, second)
            ty, tx = spot(q, to_first, to_second)
            rws = span(q, part)
            dst = out.at[sy, sx, c, rws]
            cp = remote(r.h_ref.at[rws] if own else dst, dst, r.ag_send.at[l, grp], r.ag_recv.at[l, idx], (z, ty, tx, c))
            cp.start()
            copies[idx] = cp

        def die(q, first, second, own=False):
            sy, sx = spot(q, first, second)
            rws = span(q, None)
            dst = out.at[sy, sx, c, rws]
            off = (second if q == 0 else first) % RING
            remote(r.h_ref.at[rws] if own else dst, dst, r.ag_dsend.at[l], r.ag_drecv.at[l, off], partner).start()

        def p1(q, d):
            return q * 20 + d

        def p1f(q, d):
            return q * 20 + 2 + d

        def p2(q, k, d):
            return q * 20 + 4 + k * 4 + d

        def p2f(q, k, d):
            return q * 20 + 4 + k * 4 + 2 + d

        offs = (0, -1, 1, 2)
        for q in range(2):
            for d in range(2):
                ici(p1(q, d), 0, q, 0, 0, None, SIGN[d], 0, own=True)
        for q in range(2):
            for d in range(2):
                ici(p2(q, 0, d), 1, q, 0, 0, None, 0, SIGN[d], own=True)
        for q in range(2):
            die(q, 0, 0, own=True)
        own = pltpu.make_async_copy(r.h_ref, out.at[y, x, c], r.ag_loc)
        own.start()
        hook(pump, 0)
        for d in range(2):
            for q in range(2):
                copies[p1(q, d)].wait_recv()
                src = -SIGN[d]
                ici(p1f(q, d), 2, q, src, 0, d, SIGN[d], 0)
                for e in range(2):
                    ici(p2(q, 1 + d, e), 1, q, src, 0, None, 0, SIGN[e])
                die(q, src, 0)
        hook(pump, 1)
        for d in range(2):
            for q in range(2):
                copies[p2(q, 0, d)].wait_recv()
                src = -SIGN[d]
                ici(p2f(q, 0, d), 3, q, 0, src, d, 0, SIGN[d])
                die(q, 0, src)
        hook(pump, 2)
        for q in range(2):
            copies[p1f(q, 0)].wait_recv()
            copies[p1f(q, 1)].wait_recv()
            for e in range(2):
                ici(p2(q, 3, e), 1, q, 2, 0, None, 0, SIGN[e])
            die(q, 2, 0)
        hook(pump, 3)
        for k in (1, 2, 3):
            for d in range(2):
                for q in range(2):
                    copies[p2(q, k, d)].wait_recv()
                    src = -SIGN[d]
                    ici(p2f(q, k, d), 3, q, offs[k], src, d, 0, SIGN[d])
                    die(q, offs[k], src)
            hook(pump, 3 + k)
        for k in range(4):
            for q in range(2):
                copies[p2f(q, k, 0)].wait_recv()
                copies[p2f(q, k, 1)].wait_recv()
                die(q, offs[k], 2)
        hook(pump, 7)
        for off in range(RING):
            got = out.at[turn(y, off), :, 1 - c]
            remote(got, got, r.ag_dsend.at[l], r.ag_drecv.at[l, off], partner).wait_recv()
        sent = (out.at[0, 0], out.at[0], out.at[0, 0, 0], out.at[0, pl.ds(0, 2)])
        for grp in range(4):
            remote(sent[grp], sent[grp], r.ag_send.at[l, grp], r.ag_recv.at[l, 0], partner).wait_send()
        remote(out.at[pl.ds(0, 2)], out.at[pl.ds(0, 2)], r.ag_dsend.at[l], r.ag_drecv.at[l, 0], partner).wait_send()
        own.wait()

    def h_copy(l, s, slot):
        return pltpu.make_async_copy(r.h_all.at[l, s], r.hb.at[slot], r.h_sem.at[slot])

    def h_tile(slot):
        return r.hb[slot].reshape(seq_len, d_model)

    def project(h, lo, n):
        w = r.wv[:, :, lo:lo + n].reshape(d_model, n)
        return jnp.dot(h, w, preferred_element_type=F32).astype(BF)

    def rope(val):
        val = val.astype(F32)
        return val * r.cos[...] + pltpu.roll(val, head_dim // 2, 1) * r.sin[...]

    n_chunk = min(256, f_loc)

    def kv_out_copy(l, s, slot, i):
        return pltpu.make_async_copy(r.qkv.at[slot, i], r.kv_out.at[l, i, s], r.kvo_sem.at[slot, i])

    def pass_one(l, pump):
        h_copy(l, 0, 0).start()

        @pl.loop(0, RING)
        def _(s):
            slot = lax.rem(s, 2)
            h_copy(l, s, slot).wait()

            @pl.when(s + 1 < RING)
            def _():
                h_copy(l, s + 1, 1 - slot).start()

            pump(s)

            @pl.when(s >= 2)
            def _():
                for i in range(2):
                    kv_out_copy(l, s - 2, slot, i).wait()

            kv = jnp.zeros((seq_len, 2 * head_dim), F32)
            for zz in range(RING):
                for yy in range(RING):
                    col = (zz * RING + yy) * d_row
                    kv += lax.dot_general(h_cols(slot, col, d_row), r.kvb[yy, zz], (((1,), (1,)), ((), ())), preferred_element_type=F32)
            kv = kv.astype(BF)
            r.qkv[slot, 0] = rope(kv[:, :head_dim]).astype(BF)
            r.qkv[slot, 1] = kv[:, head_dim:]
            for i in range(2):
                kv_out_copy(l, s, slot, i).start()
            q = project(h_tile(slot), 0, head_dim)
            r.stage[...] = (rope(q) * head_dim ** -0.5).astype(BF)
            for lo in range(0, f_loc, n_chunk):
                r.joined[s, :, head_dim + lo:head_dim + lo + n_chunk] = project(h_tile(slot), head_dim + lo, n_chunk)
            n_tile = seq_len // 2
            for i in range(2):
                keys = (i + 1) * n_tile
                sc = lax.dot_general(r.stage[i * n_tile:(i + 1) * n_tile, :], r.qkv[slot, 0, :keys, :], (((1,), (1,)), ((), ())), preferred_element_type=F32)
                row_id = lax.broadcasted_iota(jnp.int32, sc.shape, 0) + i * n_tile
                col_id = lax.broadcasted_iota(jnp.int32, sc.shape, 1)
                sc = jnp.where(col_id <= row_id, sc, -1e30)
                top = jnp.max(sc, axis=-1, keepdims=True)
                ex = jnp.exp(sc - top)
                prob = (ex * (1.0 / jnp.sum(ex, axis=-1, keepdims=True))).astype(BF)
                att = jnp.dot(prob, r.qkv[slot, 1, :keys, :], preferred_element_type=F32)
                r.joined[s, i * n_tile:(i + 1) * n_tile, :head_dim] = att.astype(BF)

        for s in (RING - 2, RING - 1):
            for i in range(2):
                kv_out_copy(l, s, s % 2, i).wait()

    def h_cols(slot, col, n):
        return r.hb[slot, :, :, :, col:col + n].reshape(seq_len, n)

    def pass_two(l, pump):
        h_copy(l, 0, 0).start()

        @pl.loop(0, RING)
        def _(s):
            slot = lax.rem(s, 2)
            h_copy(l, s, slot).wait()

            @pl.when(s + 1 < RING)
            def _():
                h_copy(l, s + 1, 1 - slot).start()

            pump(s)
            for lo in range(0, f_loc, n_chunk):
                up = project(h_tile(slot), head_dim + f_loc + lo, n_chunk).astype(F32)
                cols = slice(head_dim + lo, head_dim + lo + n_chunk)
                g = r.joined[s, :, cols].astype(F32)
                r.joined[s, :, cols] = (g * jax.nn.sigmoid(g) * up).astype(BF)

    def out_scatter(l, pump):
        hid = r.hid_in if l == 0 else r.hid_out

        def peer(q, first, second):
            dy = first * (1 - q) + second * q
            dx = first * q + second * (1 - q)
            return (z, turn(y, dy), turn(x, dx), c)

        def die_copy(q, s):
            return remote(r.away.at[q], r.die_in.at[q, s], r.dsend.at[l, q, s], r.drecv.at[l, q, s], partner)

        def first_copy(q, d):
            return remote(r.acc.at[q, 0, pl.ds(2 * d, 2)], r.in1.at[q, d], r.send1.at[l, q, d], r.recv1.at[l, q, d], peer(q, 1 - 2 * d, 0))

        def second_copy(q, d, h):
            return remote(r.acc.at[q, 1 + d, pl.ds(2 * h, 2)], r.in2.at[q, d, pl.ds(2 * h, 2)], r.send2.at[l, q, d, h], r.recv2.at[l, q, d, h], peer(q, 1 - 2 * d, 0))

        def third_copy(q, d):
            rws = pl.ds(d * (rows // 2), rows // 2)
            return remote(r.acc.at[q, 3, 0, rws], r.in3.at[q, d], r.send3.at[l, q, d], r.recv3.at[l, q, d], peer(q, 0, 1 - 2 * d))

        def fourth_copy(q, d):
            return remote(r.acc.at[q, 3, 1 + d], r.in4.at[q, d], r.send4.at[l, q, d], r.recv4.at[l, q, d], peer(q, 0, 1 - 2 * d))

        n_blk = r.wov.shape[3]
        blk_z = RING // 2

        def tile(q, s):
            for cc in range(CORES):
                for j in range(RING):
                    oy = SLOT_OFF[s] * (1 - q) + SLOT_OFF[j] * q
                    ox = SLOT_OFF[j] * (1 - q) + SLOT_OFF[s] * q
                    core = (1 - c) if cc == 0 else c
                    at = pl.multiple_of((turn(x, ox) * CORES + core) * rows, rows)
                    r.lhs[pl.ds((cc * RING + j) * rows, rows), :] = r.joined[turn(y, oy), pl.ds(at, rows), :]
            left = r.lhs[...]

            @pl.loop(0, half // n_blk)
            def _(n):
                col = pl.multiple_of(n * n_blk, n_blk)
                w = r.wov[q * blk_z + n // RING, lax.rem(n, RING)]
                res = jnp.dot(left, w, preferred_element_type=F32).astype(BF)
                res = res.reshape(CORES, RING, rows, n_blk)
                r.away[q, :, :, pl.ds(col, n_blk)] = res[0]
                r.acc[q, s, :, :, pl.ds(col, n_blk)] = res[1]

        def pair_sum(q, s):
            die_copy(q, s).wait_recv()

            @pl.loop(0, RING)
            def _(j):
                r.acc[q, s, j] = r.acc[q, s, j] + r.die_in[q, s, j]

        for s in range(RING):
            @pl.loop(0, 2)
            def _(q, s=s):
                if s > 0:
                    die_copy(q, s - 1).wait_send()
                tile(q, s)
                die_copy(q, s).start()
                if s > 0:
                    pair_sum(q, s - 1)
                if s == 1:
                    first_copy(q, 0).start()
                    first_copy(q, 1).start()
                if s == 2:
                    second_copy(q, 0, 1).start()
                if s == 3:
                    second_copy(q, 1, 0).start()
            pump(s)

        for q in range(2):
            pair_sum(q, 3)
        for q in range(2):
            first_copy(q, 0).wait_recv()
            for j in range(2):
                r.acc[q, 1, j] = r.acc[q, 1, j] + r.in1[q, 0, j]
            second_copy(q, 0, 0).start()
            first_copy(q, 1).wait_recv()
            for j in range(2):
                r.acc[q, 2, 2 + j] = r.acc[q, 2, 2 + j] + r.in1[q, 1, j]
            second_copy(q, 1, 1).start()
        hook(pump, 4)

        def total(q, j):
            val = r.acc[q, 3, j].astype(F32) + r.in2[q, 0, j].astype(F32) + r.in2[q, 1, j].astype(F32)
            r.acc[q, 3, j] = val.astype(BF)

        for q in range(2):
            second_copy(q, 0, 1).wait_recv()
            second_copy(q, 1, 0).wait_recv()
        hook(pump, 5)
        for q in range(2):
            second_copy(q, 0, 0).wait_recv()
            second_copy(q, 1, 1).wait_recv()
            total(q, 0)
            third_copy(q, 0).start()
            third_copy(q, 1).start()
            for j in (1, 2, 3):
                total(q, j)
        hrow = rows // 2
        for q in range(2):
            third_copy(q, 0).wait_recv()
            r.acc[q, 3, 1, pl.ds(0, hrow)] = r.acc[q, 3, 1, pl.ds(0, hrow)] + r.in3[q, 0]
            fourth_copy(q, 0).start()
            third_copy(q, 1).wait_recv()
            r.acc[q, 3, 2, pl.ds(hrow, hrow)] = r.acc[q, 3, 2, pl.ds(hrow, hrow)] + r.in3[q, 1]
            fourth_copy(q, 1).start()
        hook(pump, 6)
        for q in range(2):
            fourth_copy(q, 0).wait_recv()
            fourth_copy(q, 1).wait_recv()
            cols = pl.ds(q * half, half)
            upd = r.acc[q, 3, 3].astype(F32) + r.in4[q, 0].astype(F32) + r.in4[q, 1].astype(F32)
            upd = upd.astype(BF)
            r.hid_out[:, cols] = (hid[:, cols].astype(F32) + upd.astype(F32)).astype(BF)
        for q in range(2):
            die_copy(q, 3).wait_send()
            for d in range(2):
                first_copy(q, d).wait_send()
                second_copy(q, d, 0).wait_send()
                second_copy(q, d, 1).wait_send()
                third_copy(q, d).wait_send()
                fourth_copy(q, d).wait_send()

    def z_all(t):
        for j in (1, 2, 3):
            z_direct(t, j)

    def f_all(t):
        for j in range(RING):
            z_forward(t, j)

    def when_j(s, fn):
        @pl.when(s < 3)
        def _():
            fn(s + 1)

    with jax.named_scope("start"):
        kv_z()
        y_send(0)
        z_own(0)

    def ag0(i):
        if i == 0:
            y_send(1)
        if i == 1:
            kv_y()
            z_direct(0, 3)
            z_direct(0, 1)
        if i == 2:
            z_direct(0, 2)
            z_own(1)
        if i == 3:
            z_forward(0, 0)
            kv_x()
        if i == 4:
            z_forward(0, 3)
            z_forward(0, 1)
            z_direct(1, 3)
            z_direct(1, 1)
        if i == 5:
            z_forward(0, 2)
            z_direct(1, 2)
        if i == 6:
            y_send(2)
            z_forward(1, 0)
            kv_die(0)
        if i == 7:
            finish(0)
            kv_load(0)
            z_forward(1, 3)
            z_own(2)

    with jax.named_scope("gather_0"):
        gather_norm(0, ag0)
    with jax.named_scope("wait_w0"):
        loaded(0)
        kv_loaded()
    with jax.named_scope("fwd_1"):
        z_forward(1, 1)
        z_forward(1, 2)
        y_send(3)
    with jax.named_scope("pass_one_0"):
        pass_one(0, lambda s: when_j(s, lambda j: z_direct(2, j)))
    with jax.named_scope("finish_1"):
        finish(1)
        z_own(3)
        y_send(4)
        loaded(1)
    with jax.named_scope("pass_two_0"):
        pass_two(0, lambda s: z_forward(2, s))
    with jax.named_scope("finish_2"):
        finish(2)
        z_all(3)
        loaded(2)

    def rs0(i):
        if i == 0:
            z_forward(3, 0)
            z_forward(3, 1)
        if i == 1:
            z_forward(3, 2)
            z_forward(3, 3)
        if i == 2:
            y_send(5)
            z_own(4)
            z_direct(4, 3)
            z_direct(4, 1)
            z_direct(4, 2)
        if i == 4:
            finish(3)
            z_forward(4, 0)
            kv_die(1)
        if i == 5:
            z_forward(4, 1)
            kv_load(1)
        if i == 6:
            z_forward(4, 2)
            z_forward(4, 3)

    with jax.named_scope("scatter_0"):
        out_scatter(0, rs0)

    def ag1(i):
        if i == 1:
            z_own(5)
            z_direct(5, 3)
            z_direct(5, 1)
            z_direct(5, 2)
        if i == 4:
            finish(4)
        if i == 5:
            z_forward(5, 0)
            z_forward(5, 1)
        if i == 6:
            z_forward(5, 2)
            z_forward(5, 3)

    with jax.named_scope("gather_1"):
        gather_norm(1, ag1)
    with jax.named_scope("wait_w3"):
        loaded(3)
        kv_loaded()
    with jax.named_scope("pass_one_1"):
        pass_one(1, lambda s: None)
    with jax.named_scope("finish_5"):
        loaded(4)
        finish(5)
    with jax.named_scope("pass_two_1"):
        pass_two(1, lambda s: None)
    with jax.named_scope("wait_w5"):
        loaded(5)
    with jax.named_scope("scatter_1"):
        out_scatter(1, lambda i: None)
    with jax.named_scope("drain"):
        for t in range(3 * n_layers):
            drain(t)


def run_model(hidden, gain, wkv_t, w_in, w_out, cos_full, sin_full, seqs):
    rows, d_model = hidden.shape
    n_layers, d_row, e_block = w_in.shape
    r_block, d_col = w_out.shape[1:]
    seq_len, head_dim = cos_full.shape
    e_loc, r_loc = e_block // RING, r_block // RING
    kc = wkv_t.shape[1]
    half = d_model // 2
    dma = pltpu.SemaphoreType.DMA
    any_spec = pl.BlockSpec(memory_space=pl.ANY)
    vm_spec = pl.BlockSpec(memory_space=pltpu.VMEM)
    n_t = 3 * n_layers
    out_shape = [
        jax.ShapeDtypeStruct((rows, d_model), BF),
        jax.ShapeDtypeStruct((n_layers, 2, seqs, seq_len, head_dim), BF),
        jax.ShapeDtypeStruct((n_layers, RING, RING, CORES, rows, d_model), BF),
        jax.ShapeDtypeStruct((n_layers, RING, RING * d_row, e_loc), BF),
        jax.ShapeDtypeStruct((n_layers, RING, RING, r_loc, d_col), BF),
        jax.ShapeDtypeStruct((RING, CORES, n_layers, RING, RING, kc, d_row), BF),
    ]
    scratch = [
        pltpu.VMEM((rows, d_model), BF),
        pltpu.VMEM((RING, RING * d_row, e_loc), BF),
        pltpu.VMEM((RING, RING, 2 * head_dim, d_row), BF),
        pltpu.VMEM((RING, RING, r_loc, d_col), BF),
        pltpu.VMEM((2, RING, CORES, rows, d_model), BF),
        pltpu.VMEM((RING, seq_len, r_loc), BF),
        pltpu.VMEM((2, 2, seq_len, head_dim), BF),
        pltpu.VMEM((seq_len, head_dim), BF),
        pltpu.VMEM((CORES * RING * rows, r_loc), BF),
        pltpu.VMEM((2, RING, rows, half), BF),
        pltpu.VMEM((2, RING, RING, rows, half), BF),
        pltpu.VMEM((2, RING, RING, rows, half), BF),
        pltpu.VMEM((2, 2, 2, rows, half), BF),
        pltpu.VMEM((2, 2, RING, rows, half), BF),
        pltpu.VMEM((2, 2, rows // 2, half), BF),
        pltpu.VMEM((2, 2, rows, half), BF),
        dma((n_layers, 4)), dma((n_layers, 40)), dma((n_layers,)), dma((n_layers, RING)), dma, dma((2,)), dma((2, 2)), dma((3,)),
        dma((n_t, RING)), dma((n_t, RING, 2)), dma((n_t, RING, 2)), dma((n_t, 3)),
        dma((3,)), dma((3,)), dma((3,)), dma((3,)), dma((n_layers, 3)), dma((n_layers, 3)), dma((n_layers, 4)), dma((n_layers, 4)), dma((2,)),
        dma((n_layers, 2, RING)), dma((n_layers, 2, RING)),
        dma((n_layers, 2, 2)), dma((n_layers, 2, 2)),
        dma((n_layers, 2, 2, 2)), dma((n_layers, 2, 2, 2)),
        dma((n_layers, 2, 2)), dma((n_layers, 2, 2)),
        dma((n_layers, 2, 2)), dma((n_layers, 2, 2)),
    ]
    out = pl.pallas_call(
        model_kernel,
        out_shape=out_shape,
        in_specs=[vm_spec, vm_spec, vm_spec, any_spec, any_spec, vm_spec, vm_spec],
        out_specs=[vm_spec] + [any_spec] * 5,
        scratch_shapes=scratch,
        compiler_params=pltpu.CompilerParams(collective_id=0, has_side_effects=True, vmem_limit_bytes=VMEM_LIMIT),
        name="two_layers",
    )(hidden, gain, wkv_t, w_in, w_out, cos_full, sin_full)
    return out[0], out[1]


def solution(mesh):
    row_size = mesh.shape["row"]
    n_col = mesh.shape["col"]
    n_z = row_size // RING
    n_y = RING
    n_x = n_col // CORES
    n_tp = n_y * n_col
    n_dev = row_size * n_col
    mesh4 = Mesh(mesh.devices.reshape(n_z, n_y, n_x, CORES), ("z", "y", "x", "core"))
    every = ("z", "y", "x", "core")
    col = ("x", "core")
    act_spec = P(None, None, every)
    w_spec = P(None, ("z", "y"), col)

    def device_fn(x_loc, gain_loc, w_in_loc, w_kv_loc, w_out_loc):
        n_layers = w_in_loc.shape[0]
        n_batch, seq_len, d_local = x_loc.shape
        d_model = d_local * n_dev
        head_dim = w_kv_loc.shape[2] * n_col // 2
        batch_loc = n_batch // n_z
        tok_loc = n_batch * seq_len // n_dev
        seq_local = seq_len // n_dev
        inv_freq = 1.0 / (10000.0 ** (jnp.arange(head_dim // 2, dtype=F32) * 2.0 / head_dim))
        angles = jnp.arange(seq_len).astype(F32)[:, None] * inv_freq[None, :]
        cos_tab, sin_tab = jnp.cos(angles), jnp.sin(angles)
        cos_full = jnp.concatenate([cos_tab, cos_tab], axis=1)
        sin_full = jnp.concatenate([-sin_tab, sin_tab], axis=1)

        send = jnp.concatenate([
            x_loc.reshape(n_dev, tok_loc, d_local),
            jnp.broadcast_to(gain_loc[None], (n_dev, n_layers, d_local)),
        ], axis=1)
        got = lax.all_to_all(send, every, 0, 0, tiled=True)
        got = got.transpose(1, 0, 2).reshape(tok_loc + n_layers, d_model)
        hidden, kv = run_model(got[:tok_loc], got[tok_loc:], w_kv_loc.transpose(0, 2, 1), w_in_loc, w_out_loc, cos_full, sin_full, batch_loc)

        y_parts = hidden.reshape(tok_loc, n_dev, d_local).transpose(1, 0, 2)
        y_loc = lax.all_to_all(y_parts, every, 0, 0, tiled=True).reshape(n_batch, seq_len, d_local)
        kv = kv.reshape(n_layers, 2, batch_loc, n_z, n_tp, seq_local, head_dim)
        me = (lax.axis_index("y") * n_x + lax.axis_index("x")) * CORES + lax.axis_index("core")
        kv = lax.dynamic_index_in_dim(kv, me, axis=4, keepdims=False)
        kv = lax.all_to_all(kv, "z", 3, 2, tiled=True)
        kv = kv.reshape(n_layers, 2, n_batch, seq_local, head_dim)
        return y_loc, kv

    return jax.shard_map(device_fn, mesh=mesh4, in_specs=(act_spec, P(None, every), w_spec, w_spec, P(None, col, ("z", "y"))), out_specs=(act_spec, P(None, None, None, every, None)), check_vma=False)
```

time: 2660 us -> 449 us (0.17)
  waiting for transfers between devices: 1750 us -> 31 us
  Pallas kernels: 0 us -> 376 us
  other arithmetic: 283 us -> 2.6 us
  blocking collectives: 262 us -> 0 us
  matrix products: 229 us -> 0 us
  local copies, waits for them, and re-layouts: 112 us -> 14.7 us
    psum x2 -> x0, waiting for transfers between devices: 1630 us -> none  [device_fn(): main_proj, kv_piece = lax.psum((part_main, part_kv), 'row')]
    pallas_call x0 -> x1, Pallas kernels: none -> 376 us  [run_model(): pl.pallas_call(model_kernel, out_shape=out_shape, in_specs=[vm_spec, vm_s...]
    psum x4 -> x0, blocking collectives: 262 us -> none  [the longest x2 137 us: device_fn(): lax.psum(jnp.sum(hidden_f32, axis=-1, keepdims=True), ('row', 'col'))]
    dot_general x10 -> x0, matrix products: 229 us -> none  [the longest x2 68.5 us: device_fn(): jnp.einsum('crie,cle->cirl', q_rot, k_rot, preferred_element_type=jnp.flo...]
    sub x6 -> x0, other arithmetic: 168 us -> none  [the longest x2 132 us: device_fn(): attn_prob = jax.nn.softmax(scores, axis=-1).astype(jnp.bfloat16)]
    convert_element_type x8 -> x1, other arithmetic: 95 us -> 0.01 us  [device_fn(): angles = jnp.arange(seq_len).astype(F32)[:, None] * inv_freq[None, :]]
    reduce_scatter x2 -> x0, waiting for transfers between devices: 62.8 us -> none  [device_fn(): update = lax.psum_scatter(part_out, 'col', scatter_dimension=2, tiled=True)]
    all_gather x4 -> x0, waiting for transfers between devices: 59 us -> none  [the longest x2 58.9 us: device_fn(): normed_row = lax.all_gather(normed, 'col', axis=2, tiled=True)]
  transfers between devices with their start and end apart: 8 -> 3, of which waited for: 6 -> 3; matrix products, arithmetic and copies ran while one was open for 8% -> 1% of each run, Pallas kernels for 0% -> 0%
where the time goes in v3:
time: 449 us; the launch traced here: 448 us
  Pallas kernels  376 us (84%)
  waiting for transfers between devices  31 us (7%)
  starting transfers between devices  23.2 us (5%)
  local copies, waits for them, and re-layouts  14.7 us (3%)
    pallas_call x1, Pallas kernels, run_model(): pl.pallas_call(model_kernel, out_shape=out_shape, in_specs=[vm_spec, vm_s...  376 us
    all_to_all x1, waiting for transfers between devices, device_fn(): got = lax.all_to_all(send, every, 0, 0, tiled=True)  17 us
    all_to_all x1, waiting for transfers between devices, device_fn(): lax.all_to_all(y_parts, every, 0, 0, tiled=True)  12.7 us
    all_to_all x1, starting transfers between devices, device_fn(): got = lax.all_to_all(send, every, 0, 0, tiled=True)  11.5 us
  transfers between devices with their start and end apart: 3, of which 3 were waited for; matrix products, arithmetic and copies ran while one was open for 1% of the time, Pallas kernels for 0%

profile of v3, /device:TPU:1, one launch (start us, length us, event | category | flops | bytes accessed | tf_op | source)
XLA Modules:
  0.0 448.3 jit_solution(343381400192858054)
XLA Ops:
  0.6 0.8 copy.28
  1.4 1.3 copy.27
  2.7 0.5 reshape.34
  3.2 0.1 broadcast_in_dim.2
  3.4 0.6 pad_maximum_fusion
  4.0 1.6 copy.29
  5.6 11.5 %all-to-all-start = ((bf16[128,66,32]{1,2,0:T(8,128)(2,1)}), bf16[128,66,32]{1,2,0:T(8,128)(2,1)S(1)}, u32[]{:S(2)}, u32[]{:S(2)}) async-start(bf16[128,66,32]{1,2,0:T(8,128)(2,1)} %copy.29), calls=%async_computation | async-start | bytes 2097152 | tf_op jit(solution)/shard_map/all_to_all | solution.py:777
  17.2 1.0 fusion
  18.2 1.0 pad_maximum_fusion.1
  19.2 17.0 %all-to-all-done = bf16[128,66,32]{1,2,0:T(8,128)(2,1)S(1)} async-done(((bf16[128,66,32]{1,2,0:T(8,128)(2,1)}), bf16[128,66,32]{1,2,0:T(8,128)(2,1)S(1)}, u32[]{:S(2)}, u32[]{:S(2)}) %all-to-all-start) | async-done | bytes 540704 | tf_op jit(solution)/shard_map/all_to_all | solution.py:777
  36.2 0.4 slice.17
  36.5 1.1 copy.31.refs_0_
  37.6 1.0 copy.39.refs_1_
  38.6 376.0 %two_layers.1 = (bf16[64,4096]{1,0:T(8,128)(2,1)}, bf16[2,2,4,512,128]{4,3,2,1,0:T(8,128)(2,1)}, bf16[2,4,4,2,64,4096]{5,4,3,2,1,0:T(8,128)(2,1)}, bf16[2,4,1024...) custom-call(bf16[64,4096]{1,0:T(8,128)(2,1)} %copy.31.refs_0_, ...), custom_call_target="tpu_custom_call" | custom-call | tf_op jit(solution)/shard_map/two_layers/pallas_call | solution.py:733
  414.6 0.9 dynamic-slice_bitcast_fusion
  415.5 0.7 copy.35
  416.2 3.8 all-to-all-start.2
  420.0 1.5 copy.32
  421.5 1.4 reshape.39
  422.9 1.4 all-to-all-done.2
  424.2 8.0 %all-to-all-start.1 = ((bf16[128,2,1024]{2,1,0:T(2,128)(2,1)}), bf16[128,2,1024]{2,1,0:T(2,128)(2,1)S(1)}, u32[]{:S(2)}, u32[]{:S(2)}) async-start(bf16[128,2,1024]{2,1,0:T(2,128)(2,1)} %reshape.39), calls=%async_computation.1 | async-start | bytes 1048576 | tf_op jit(solution)/shard_map/all_to_all | solution.py:782
  432.2 0.7 copy.38
  432.9 12.7 %all-to-all-done.1 = bf16[128,2,1024]{2,1,0:T(2,128)(2,1)S(1)} async-done(((bf16[128,2,1024]{2,1,0:T(2,128)(2,1)}), bf16[128,2,1024]{2,1,0:T(2,128)(2,1)S(1)}, u32[]{:S(2)}, u32[]{:S(2)}) %all-to-all-start.1) | async-done | bytes 524320 | tf_op jit(solution)/shard_map/all_to_all | solution.py:782
  445.6 0.6 reshape.40
  446.2 0.4 copy.33
  446.6 0.6 reshape.36
  447.2 1.1 copy.37
  (3 shorter events, 0.0 us)
Async XLA Ops:
  5.6 30.5 %all-to-all-start = ((bf16[128,66,32]{1,2,0:T(8,128)(2,1)}), bf16[128,66,32]{1,2,0:T(8,128)(2,1)S(1)}, u32[]{:S(2)}, u32[]{:S(2)}) async-start(bf16[128,66,32]{1,2,0:T(8,128)(2,1)} %copy.29), calls=%async_computation | async-start | bytes 2097152 | tf_op jit(solution)/shard_map/all_to_all | solution.py:777
  416.2 8.0 %all-to-all-start.2 = ((bf16[2,2,4,4,4,128]{5,4,2,1,0,3:T(4,128)(2,1)}), bf16[2,2,4,4,4,128]{5,4,2,1,0,3:T(4,128)(2,1)S(1)}, u32[]{:S(2)}, u32[]{:S(2)}) async-start(bf16[2,2,4,4,4,128]{5,4,2,1,0,3:T(4,128)(2,1)} %copy.35), calls=%async_computation.2 | async-start | bytes 131072 | tf_op jit(solution)/shard_map/all_to_all | solution.py:786
  424.2 21.4 %all-to-all-start.1 = ((bf16[128,2,1024]{2,1,0:T(2,128)(2,1)}), bf16[128,2,1024]{2,1,0:T(2,128)(2,1)S(1)}, u32[]{:S(2)}, u32[]{:S(2)}) async-start(bf16[128,2,1024]{2,1,0:T(2,128)(2,1)} %reshape.39), calls=%async_computation.1 | async-start | bytes 1048576 | tf_op jit(solution)/shard_map/all_to_all | solution.py:782
